TPU v7x, 32 devices: a whole 2x2x4 slice. The times are simulated.
32 devices in a mesh: dp: 16 (over z, y, x), mp: 2 (over core).
Axes of the slice: x: 2, y: 2, z: 4, core: 2. Of those that a mesh axis runs over, the one named last changes fastest.
Arguments:
- points: bfloat16 [16384, 1024], P(('dp', 'mp')), may hold values from -6 to 6
- centroids: bfloat16 [4096, 1024], P('mp'), may hold values from -6 to 6
- assign: int32 [16384], P(('dp', 'mp')), may hold values from 0 to 4095
- keep_mask: int32 [16384], P(('dp', 'mp')), may hold values 0 or 1
Outputs:
- new_centroids: float32 [4096, 1024], P('mp')
- row_cost: float32 [16384], P(('dp', 'mp'))
All inputs are finite; a program needn't handle non-finite values. No bound on the sum of `keep_mask` on one device may be relied on, other than what follows from the above.
Results may differ from a plain program's by a relative error of at most 0.0008.
Values may be sent and summed in bfloat16 or wider, within the bound.
No kernel may reach another device: no remote copies, remote signals or barrier semaphores. Data moves between devices by JAX's collectives and lax.ppermute only.
A program may use at most 128 MiB of HBM per device.

v0:
```python
import functools

import jax
import jax.numpy as jnp
from jax import lax
from jax.experimental import pallas as pl
from jax.experimental.pallas import tpu as pltpu
from jax.sharding import Mesh, PartitionSpec as P


LANES = 128
COLS = 64
LOW = 4
DIGIT = 7
CODE_ROWS = 16
LEVELS = 32767.0
TINY = 1e-30
GROUP = 8
SMALL_VMEM = 24 << 20
F32, BF16, I32 = jnp.float32, jnp.bfloat16, jnp.int32
HALF = LANES // 2
SWAP = [(0, 1), (1, 0)]
OWNERS = ("z", "y", "x")
AXES = ("g",) + OWNERS + ("mp",)

VMEM = pl.BlockSpec(memory_space=pltpu.VMEM)
SMEM = pl.BlockSpec(memory_space=pltpu.SMEM)


def pack_kernel(points_ref, assign_ref, keep_ref, out_ref):
    rows, width = points_ref.shape
    blocks = rows // LANES
    kept = keep_ref[...]
    assign = assign_ref[...]
    high = jnp.where(kept > 0, assign >> DIGIT, -1).astype(F32)
    low = (assign & ((1 << DIGIT) - 1)).astype(F32)
    weight = kept.astype(F32)
    peak = jnp.zeros((1, LANES), F32)
    for b in range(blocks):
        for c in range(width // LANES):
            tile = points_ref[b * LANES : (b + 1) * LANES, c * LANES : (c + 1) * LANES].T
            out_ref[2 * c, b * COLS : (b + 1) * COLS, :] = tile[:COLS]
            out_ref[2 * c + 1, b * COLS : (b + 1) * COLS, :] = tile[COLS:]
            size = jnp.max(jnp.abs(tile.astype(F32)), axis=0, keepdims=True)
            peak = jnp.maximum(peak, size * weight[b : b + 1])
    pad = jnp.zeros((CODE_ROWS - 2 * blocks - 1, LANES), F32)
    codes = jnp.concatenate([high, low, peak, pad], axis=0).astype(BF16)
    for s in range(out_ref.shape[0]):
        out_ref[s, blocks * COLS :, :] = codes


def pack(points, assign, keep):
    rows, width = points.shape
    blocks = rows // LANES
    assert 2 * blocks + 1 <= CODE_ROWS
    shape = (width // COLS, blocks * COLS + CODE_ROWS, LANES)
    return pl.pallas_call(
        pack_kernel,
        out_shape=jax.ShapeDtypeStruct(shape, BF16),
        in_specs=[VMEM] * 3,
        out_specs=VMEM,
        cost_estimate=pl.CostEstimate(
            flops=2 * rows * width, bytes_accessed=4 * rows * width, transcendentals=0
        ),
        name="pack",
    )(points, assign.reshape(blocks, LANES), keep.reshape(blocks, LANES))


def add_sources(base, recv_ref, acc_ref):
    sources, height, _ = recv_ref.shape
    high_size = acc_ref.shape[1]
    blocks = (height - CODE_ROWS) // COLS
    rows = blocks * LANES
    shift = high_size.bit_length() - 1

    group = min(GROUP, sources)

    def factors(s):
        codes = recv_ref[s, blocks * COLS :, :].astype(F32)
        local = (codes[:blocks] * float(1 << DIGIT) + codes[blocks : 2 * blocks]).astype(I32) - base
        local = jnp.concatenate([local[b : b + 1] for b in range(blocks)], axis=1)
        k_low, k_high = local >> shift, local & (high_size - 1)
        hot = (lax.broadcasted_iota(I32, (high_size, rows), 0) == k_high).astype(F32).astype(BF16)
        data = [recv_ref[s, b * COLS : (b + 1) * COLS, :] for b in range(blocks)]
        data = jnp.concatenate(data, axis=1)
        masks = [(k_low == l).astype(F32) for l in range(LOW)]
        parts = [data * m.astype(BF16) for m in masks]
        pad = jnp.zeros((CODE_ROWS - LOW, rows), F32)
        parts.append(jnp.concatenate(masks + [pad], axis=0).astype(BF16))
        return jnp.concatenate(parts, axis=0), hot, codes[2 * blocks : 2 * blocks + 1]

    def step(i, peak):
        left, hot, size = zip(*[factors(i * group + u) for u in range(group)])
        left, hot = jnp.concatenate(left, axis=1), jnp.concatenate(hot, axis=1)
        acc_ref[...] += lax.dot_general(
            left, hot, (((1,), (1,)), ((), ())), preferred_element_type=F32
        )
        return functools.reduce(jnp.maximum, size, peak)

    return lax.fori_loop(0, sources // group, step, jnp.zeros((1, LANES), F32))


def finish(where_ref, acc_ref, scale, prior_ref, out_ref):
    high_size = acc_ref.shape[1]
    counts = acc_ref[LOW * COLS : LOW * COLS + 8, :]
    inverse = 1.0 / jnp.maximum(counts, 1.0)
    tall = counts.T
    odd = where_ref[1] > 0
    lower = lax.broadcasted_iota(I32, (high_size, LANES), 1) < HALF
    for l in range(0, LOW, 2):
        mean = [acc_ref[k * COLS : (k + 1) * COLS, :] * inverse[k : k + 1] for k in (l, l + 1)]
        mean = jnp.concatenate(mean, axis=0).T
        priors = [prior_ref[k * high_size : (k + 1) * high_size, :].astype(F32) for k in (l, l + 1)]
        turned = [pltpu.roll(p, HALF, 1) for p in priors]
        prior = jnp.where(
            lower, jnp.where(odd, turned[0], priors[0]), jnp.where(odd, priors[1], turned[1])
        )
        count = jnp.where(lower, tall[:, l : l + 1], tall[:, l + 1 : l + 2])
        value = jnp.where(count > 0.5, mean, prior)
        root = jnp.sqrt(jnp.sqrt(jnp.abs(value) * scale))
        level = jnp.minimum(root * LEVELS + 0.5, LEVELS).astype(I32)
        level = jnp.where(value < 0, -level, level).astype(jnp.int16)
        out_ref[:, l * COLS : (l + 2) * COLS] = level


def first_kernel(where_ref, recv_ref, acc_ref, peak_ref):
    acc_ref[...] = jnp.zeros_like(acc_ref)
    peak = add_sources(where_ref[0], recv_ref, acc_ref)
    peak_ref[...] = jnp.broadcast_to(peak, peak_ref.shape)


def second_kernel(where_ref, recv_ref, given_ref, given_peak_ref, acc_ref, peak_ref):
    acc_ref[...] = given_ref[...]
    peak = add_sources(where_ref[0], recv_ref, acc_ref)
    peak_ref[...] = jnp.maximum(given_peak_ref[...], peak)


def last_kernel(where_ref, least_ref, recv_ref, given_ref, given_peak_ref, prior_ref, out_ref, peak_ref, acc_ref):
    acc_ref[...] = given_ref[...]
    peak = jnp.maximum(given_peak_ref[...], add_sources(where_ref[0], recv_ref, acc_ref))
    peak = jnp.maximum(jnp.max(peak), least_ref[0])
    peak_ref[0] = peak
    finish(where_ref, acc_ref, 1.0 / peak, prior_ref, out_ref)


def finish_kernel(where_ref, peak_ref, acc_ref, prior_ref, out_ref):
    finish(where_ref, acc_ref, 1.0 / peak_ref[0], prior_ref, out_ref)


def sums_cost(recv, high_size):
    sources, height, _ = recv.shape
    rows = (height - CODE_ROWS) // COLS * LANES * sources
    flops = 2 * rows * (LOW * COLS + CODE_ROWS) * high_size
    return pl.CostEstimate(flops=flops, bytes_accessed=recv.size * 2, transcendentals=0)


def sums_of(recv, where, given, high_size):
    shapes = (
        jax.ShapeDtypeStruct((LOW * COLS + CODE_ROWS, high_size), F32),
        jax.ShapeDtypeStruct((8, LANES), F32),
    )
    return pl.pallas_call(
        first_kernel if given is None else second_kernel,
        out_shape=shapes,
        in_specs=[SMEM, VMEM] + ([] if given is None else [VMEM, VMEM]),
        out_specs=(VMEM, VMEM),
        cost_estimate=sums_cost(recv, high_size),
        compiler_params=pltpu.CompilerParams(vmem_limit_bytes=SMALL_VMEM),
        name="sums_first" if given is None else "sums_second",
    )(where, recv, *(given or ()))


def unit_shape(high_size):
    return jax.ShapeDtypeStruct((high_size, LOW * COLS), jnp.int16)


def last_sums(recv, where, given, least, prior, high_size):
    return pl.pallas_call(
        last_kernel,
        out_shape=(unit_shape(high_size), jax.ShapeDtypeStruct((1,), F32)),
        in_specs=[SMEM, SMEM, VMEM, VMEM, VMEM, VMEM],
        out_specs=(VMEM, SMEM),
        scratch_shapes=[pltpu.VMEM(given[0].shape, F32)],
        cost_estimate=sums_cost(recv, high_size),
        compiler_params=pltpu.CompilerParams(vmem_limit_bytes=SMALL_VMEM),
        name="sums_last",
    )(where, least, recv, *given, prior)


def finished(acc, peak, prior, where):
    return pl.pallas_call(
        finish_kernel,
        out_shape=unit_shape(acc.shape[1]),
        in_specs=[SMEM, SMEM, VMEM, VMEM],
        out_specs=VMEM,
        name="finish",
    )(where, peak, acc, prior)


def spread_kernel(parts, where_ref, peak_ref, own_ref, x_piece_ref, y_piece_ref, *refs):
    out_ref = refs[-1]
    high_size = own_ref.shape[0]
    first = where_ref[1] == 0
    y = where_ref[2]

    def emit(mine_ref, at, other_ref, column):
        rows = other_ref.shape[0]
        lower = lax.broadcasted_iota(jnp.int16, (rows, LANES), 1) < HALF
        lanes = pl.ds(pl.multiple_of(column * LANES, LANES), LANES)
        mine, other = mine_ref[at : at + rows, :], other_ref[...]
        left, right = jnp.where(first, mine, other), jnp.where(first, other, mine)
        both = (
            jnp.where(lower, left, pltpu.roll(right, HALF, 1)),
            jnp.where(lower, pltpu.roll(left, HALF, 1), right),
        )
        for k, level in enumerate(both):
            t = level.astype(I32).astype(F32) * (1.0 / LEVELS)
            s = t * jnp.abs(t)
            start = k * high_size + at
            out_ref[start : start + rows, lanes] = s * jnp.abs(s) * peak_ref[0]

    emit(own_ref, 0, x_piece_ref, y)
    at = 0
    for ref in refs[:parts]:
        emit(y_piece_ref, at, ref, 1 - y)
        at += ref.shape[0]


def spread(n, own, x_piece, y_piece, diagonal, where, peak, width, into):
    high_size, _ = own.shape
    total = LOW * high_size
    pieces = [own, x_piece, y_piece, *diagonal]
    extra = [] if into is None else [into]
    return pl.pallas_call(
        functools.partial(spread_kernel, len(diagonal)),
        grid_spec=pltpu.PrefetchScalarGridSpec(
            num_scalar_prefetch=1,
            grid=(LOW // 2,),
            in_specs=[SMEM]
            + [pl.BlockSpec((p.shape[0], LANES), lambda i, w: (0, i)) for p in pieces]
            + [pl.BlockSpec(memory_space=pl.ANY) for _ in extra],
            out_specs=pl.BlockSpec((2 * high_size, 2 * LANES), lambda i, w: (i, w[3 + n])),
        ),
        out_shape=jax.ShapeDtypeStruct((total, width), F32),
        input_output_aliases={2 + len(pieces): 0} if extra else {},
        cost_estimate=pl.CostEstimate(
            flops=16 * total * LANES, bytes_accessed=12 * total * LANES, transcendentals=0
        ),
        compiler_params=pltpu.CompilerParams(vmem_limit_bytes=SMALL_VMEM),
        name="spread",
    )(where, peak, *pieces, *extra)


def z_shifts(nz):
    return [0, 1, nz - 1] + list(range(2, nz - 1))


def gather(unit, peak, where, width):
    nz = lax.axis_size("z")
    rows = unit.shape[0]
    held = [unit]
    for n, s in enumerate(z_shifts(nz)[1:], 1):
        held.append(lax.ppermute(unit, "z", [(i, (i + s) % nz) for i in range(nz)]))
    out = None
    for n, piece in enumerate(held):
        from_x = lax.ppermute(piece, "x", SWAP)
        from_y = lax.ppermute(piece, "y", SWAP)
        cut = (rows, 0)[n] if n < 2 else rows // 2
        diagonal = []
        if cut:
            diagonal.append(lax.ppermute(from_y[:cut], "x", SWAP))
        if cut < rows:
            diagonal.append(lax.ppermute(from_x[cut:], "y", SWAP))
        out = spread(n, piece, from_x, from_y, diagonal, where, peak, width, out)
    return out


def nearest(points, point_sq, part):
    inner = lax.dot_general(points, part, (((1,), (1,)), ((), ())), preferred_element_type=F32)
    part_f = part.astype(F32)
    part_sq = jnp.sum(part_f * part_f, axis=1)
    return jnp.min(point_sq[:, None] - 2.0 * inner + part_sq[None, :], axis=1)


def shards(points, centroids, assign, keep_mask):
    width = points.shape[1]
    shard_rows = centroids.shape[0]
    high_size = shard_rows // LOW
    z, y, x = (lax.axis_index(a) for a in OWNERS)
    nz, ny, nx = (lax.axis_size(a) for a in OWNERS)
    assert nx == 2 and ny == 2 and nz * ny * nx * COLS == width
    block = z * ny + y
    blocks = [(z - s) % nz for s in z_shifts(nz)]
    where = jnp.stack([lax.axis_index("mp") * shard_rows, x, y, *blocks]).astype(I32)

    parcels = pack(points, assign, keep_mask)
    recv = lax.all_to_all(parcels, OWNERS, 0, 0, tiled=True)
    others = lax.ppermute(centroids, "mp", SWAP)

    point_f = points.astype(F32)
    point_sq = jnp.sum(point_f * point_f, axis=1)
    best = jnp.minimum(nearest(points, point_sq, centroids), nearest(points, point_sq, others))
    least = jnp.maximum(jnp.max(jnp.abs(centroids)).astype(F32), TINY)[None]
    prior = lax.dynamic_slice_in_dim(centroids, block * LANES, LANES, 1)
    recv, best, least, prior, where = lax.optimization_barrier((recv, best, least, prior, where))

    partner = lax.ppermute(recv, "mp", SWAP)
    given = sums_of(recv, where, None, high_size)
    if lax.axis_size("g") > 1:
        acc, peak = sums_of(partner, where, given, high_size)
        acc, peak = lax.psum(acc, "g"), lax.pmax(jnp.max(peak), "g")
        peak = jnp.maximum(peak, least)
        unit = finished(acc, peak, prior, where)
    else:
        unit, peak = last_sums(partner, where, given, least, prior, high_size)

    out = gather(unit, peak, where, width)
    return out, best / width


def split_dp(mesh, width):
    dp, mp = mesh.shape["dp"], mesh.shape["mp"]
    owners = width // COLS
    devices = mesh.devices.reshape(dp // owners, owners // 4, 2, 2, mp)
    return Mesh(devices, AXES)


def solution(mesh):
    rows = P(AXES)

    def step(points, centroids, assign, keep_mask):
        return jax.shard_map(
            shards,
            mesh=split_dp(mesh, points.shape[1]),
            in_specs=(P(AXES, None), P("mp", None), rows, rows),
            out_specs=(P("mp", None), rows),
            check_vma=False,
        )(points, centroids, assign, keep_mask)

    return step
```

profile of v0, /device:TPU:0, one launch (start us, length us, event | category | flops | bytes accessed | tf_op | source)
XLA Modules:
  0.0 109.5 jit_solution(2505197055208168652)
XLA Ops:
  0.6 0.6 collective-permute-start
  1.2 2.7 %pack.1 = bf16[16,272,128]{2,1,0:T(8,128)(2,1)} custom-call(bf16[512,1024]{1,0:T(8,128)(2,1)} %points_ref.1, s32[4,128]{1,0:T(4,128)} %bitcast.14, s32[4,128]{1,0:T(4,128)} %bitcast.15), custom_call_target="tpu_custom_call" | custom-call | flops 1048576 | bytes 2097152 | tf_op jit(solution)/shard_map/pack/pallas_call | solution.py:57
  3.9 7.9 %all-to-all-start = ((bf16[16,272,128]{2,1,0:T(8,128)(2,1)}), bf16[16,272,128]{2,1,0:T(8,128)(2,1)S(1)}, u32[]{:S(2)}, u32[]{:S(2)}) async-start(bf16[16,272,128]{2,1,0:T(8,128)(2,1)} %pack.1), calls=%async_computation | async-start | bytes 2228224 | tf_op jit(solution)/shard_map/all_to_all | solution.py:297
  11.8 3.7 %abs_reduce_fusion = bf16[]{:T(256)} fusion(bf16[2048,1024]{1,0:T(8,128)(2,1)} %param.5), kind=kLoop, calls=%fused_computation.2 | loop fusion | flops 4194303 | bytes 4194306 | tf_op jit(solution)/shard_map/reduce_max | solution.py:303
  16.1 0.1 stack.31.where_ref
  16.2 0.3 multiply_reduce_fusion.2
  16.5 1.2 %constant_dynamic-slice_fusion.prior_ref = bf16[2048,128]{1,0:T(8,128)(2,1)S(1)} fusion(bf16[2048,1024]{1,0:T(8,128)(2,1)} %param.5, s32[]{:T(128)S(6)} %select_n.22), kind=kLoop, calls=%fused_computation.7 | loop fusion | bytes 1048580 | tf_op jit(solution)/shard_map/dynamic_slice | solution.py:304
  17.7 3.1 %multiply_reduce_fusion.1 = f32[2048]{0:T(1024)S(1)} fusion(bf16[2048,1024]{1,0:T(8,128)(2,1)} %param.5), kind=kLoop, calls=%fused_computation.1 | loop fusion | flops 6289408 | bytes 4202496 | tf_op jit(solution)/shard_map/reduce_sum | solution.py:281
  20.8 2.5 %add_reduce_fusion.1 = f32[512]{0:T(512)S(1)} fusion(bf16[512,1024]{1,0:T(8,128)(2,1)S(1)} %copy-done.1, bf16[2048,1024]{1,0:T(8,128)(2,1)S(1)} %copy-done, f32[2048]{0:T(1024)S(1)} %multiply_reduce_fusion.1, f32[512]{0:T(512)S(1)} %multiply_reduce_fusion.2), kind=kOutput, calls=%fused_computation.4 | convolution fusion | flops 2151677440 | bytes 5255168 | tf_op jit(solution)/shard_map/dot_general | solution.py:279
  23.3 0.0 collective-permute-done
  23.3 3.1 %multiply_reduce_fusion = f32[2048]{0:T(1024)S(1)} fusion(bf16[2048,1024]{1,0:T(8,128)(2,1)} %collective-permute-done), kind=kLoop, calls=%fused_computation | loop fusion | flops 6289408 | bytes 4202496 | tf_op jit(solution)/shard_map/reduce_sum | solution.py:281
  26.4 4.7 %add_reduce_fusion = f32[512]{0:T(512)S(1)} fusion(f32[2048]{0:T(1024)S(1)} %multiply_reduce_fusion, f32[512]{0:T(512)S(1)} %multiply_reduce_fusion.2, bf16[512,1024]{1,0:T(8,128)(2,1)S(1)} %copy-done.1, bf16[2048,1024]{1,0:T(8,128)(2,1)} %collective-permute-done), kind=kOutput, calls=%fused_computation.3 | convolution fusion | flops 2151677440 | bytes 5255168 | tf_op jit(solution)/shard_map/dot_general | solution.py:279
  31.1 6.7 %all-to-all-done.recv_ref = bf16[16,272,128]{2,1,0:T(8,128)(2,1)S(1)} async-done(((bf16[16,272,128]{2,1,0:T(8,128)(2,1)}), bf16[16,272,128]{2,1,0:T(8,128)(2,1)S(1)}, u32[]{:S(2)}, u32[]{:S(2)}) %all-to-all-start) | async-done | bytes 1114144 | tf_op jit(solution)/shard_map/all_to_all | solution.py:297
  37.8 3.3 %sums_first.1 = (f32[272,512]{1,0:T(8,128)S(1)}, f32[8,128]{1,0:T(8,128)S(1)}) custom-call(s32[7]{0:T(128)S(1)} %stack.31.where_ref, bf16[16,272,128]{2,1,0:T(8,128)(2,1)S(1)} %all-to-all-done.recv_ref), custom_call_target="tpu_custom_call" | custom-call | flops 2281701376 | bytes 1114112 | tf_op jit(solution)/shard_map/sums_first/pallas_call | solution.py:162
  41.1 0.0 collective-permute-done.1.recv_ref
  41.1 4.5 %sums_last.1 = (s16[512,256]{1,0:T(8,128)(2,1)S(1)}, f32[1]{0:T(128)}) custom-call(s32[7]{0:T(128)S(1)} %stack.31.where_ref, f32[1]{0:T(128)} %bitcast.2.least_ref, bf16[16,272,128]{2,1,0:T(8,128)(2,1)S(1)} %collective-permute-done.1.recv_ref, f32[272,512]{1,0:T(8,128)S(1)} %get-tuple-element.14.given_ref, f32[8,128]{1,0:T(8,128)S(1)} %get-tuple-element.15.given_peak_ref, ...), custom_call_target="tpu_custom_call" | custom-call | flops 2281701376 | bytes 1114112 | tf_op jit(solution)/shard_map/sums_last/pallas_call | solution.py:178
  45.6 3.6 %collective-permute-start.12 = (s16[512,256]{1,0:T(8,128)(2,1)S(1)}, s16[512,256]{1,0:T(8,128)(2,1)S(1)}, u32[]{:S(2)}, u32[]{:S(2)}) collective-permute-start(s16[512,256]{1,0:T(8,128)(2,1)S(1)} %get-tuple-element.18.own_ref), channel_id=1, source_target_pairs={{0,8},{8,16},{16,24},{24,0},{1,9},{9,17},{17,25},{25,1},{2,10},{10... | collective-permute-start | bytes 786440 | tf_op jit(solution)/shard_map/ppermute | solution.py:263
  49.2 0.5 collective-permute-start.7
  49.7 1.6 %collective-permute-start.2 = (s16[512,256]{1,0:T(8,128)(2,1)S(1)}, s16[512,256]{1,0:T(8,128)(2,1)S(1)}, u32[]{:S(2)}, u32[]{:S(2)}) collective-permute-start(s16[512,256]{1,0:T(8,128)(2,1)S(1)} %get-tuple-element.18.own_ref), channel_id=1, source_target_pairs={{0,16},{8,24},{16,0},{24,8},{1,17},{9,25},{17,1},{25,9},{2,18},{10... | collective-permute-start | bytes 786440 | tf_op jit(solution)/shard_map/ppermute | solution.py:263
  51.3 0.9 collective-permute-start.17
  52.2 4.4 %collective-permute-done.12.own_ref = s16[512,256]{1,0:T(8,128)(2,1)S(1)} collective-permute-done((s16[512,256]{1,0:T(8,128)(2,1)S(1)}, s16[512,256]{1,0:T(8,128)(2,1)S(1)}, u32[]{:S(2)}, u32[]{:S(2)}) %collective-permute-start.12) | collective-permute-done | bytes 262176 | tf_op jit(solution)/shard_map/ppermute | solution.py:263
  56.6 0.9 collective-permute-start.13
  57.5 4.5 %collective-permute-done.7.own_ref = s16[512,256]{1,0:T(8,128)(2,1)S(1)} collective-permute-done((s16[512,256]{1,0:T(8,128)(2,1)S(1)}, s16[512,256]{1,0:T(8,128)(2,1)S(1)}, u32[]{:S(2)}, u32[]{:S(2)}) %collective-permute-start.7) | collective-permute-done | bytes 262176 | tf_op jit(solution)/shard_map/ppermute | solution.py:263
  62.0 2.2 %collective-permute-start.9 = (s16[512,256]{1,0:T(8,128)(2,1)S(1)}, s16[512,256]{1,0:T(8,128)(2,1)S(1)}, u32[]{:S(2)}, u32[]{:S(2)}) collective-permute-start(s16[512,256]{1,0:T(8,128)(2,1)S(1)} %collective-permute-done.7.own_ref), channel_id=1, source_target_pairs={{0,4},{4,0},{1,5},{5,1},{2,6},{6,2},{3,7},{7,3},{8,12},{12,8},{9,1... | collective-permute-start | bytes 786440 | tf_op jit(solution)/shard_map/ppermute | solution.py:267
  64.2 0.7 collective-permute-start.8
  64.9 8.3 %collective-permute-done.2.own_ref = s16[512,256]{1,0:T(8,128)(2,1)S(1)} collective-permute-done((s16[512,256]{1,0:T(8,128)(2,1)S(1)}, s16[512,256]{1,0:T(8,128)(2,1)S(1)}, u32[]{:S(2)}, u32[]{:S(2)}) %collective-permute-start.2) | collective-permute-done | bytes 262176 | tf_op jit(solution)/shard_map/ppermute | solution.py:263
  73.3 2.2 %collective-permute-start.4 = (s16[512,256]{1,0:T(8,128)(2,1)S(1)}, s16[512,256]{1,0:T(8,128)(2,1)S(1)}, u32[]{:S(2)}, u32[]{:S(2)}) collective-permute-start(s16[512,256]{1,0:T(8,128)(2,1)S(1)} %collective-permute-done.2.own_ref), channel_id=1, source_target_pairs={{0,4},{4,0},{1,5},{5,1},{2,6},{6,2},{3,7},{7,3},{8,12},{12,8},{9,1... | collective-permute-start | bytes 786440 | tf_op jit(solution)/shard_map/ppermute | solution.py:267
  75.5 0.0 collective-permute-done.17.y_piece_ref
  75.5 0.7 collective-permute-start.3
  76.1 0.0 collective-permute-done.13.x_piece_ref
  76.2 1.3 %collective-permute-start.16 = (s16[512,256]{1,0:T(8,128)(2,1)S(1)}, s16[512,256]{1,0:T(8,128)(2,1)S(1)}, u32[]{:S(2)}, u32[]{:S(2)}) collective-permute-start(s16[512,256]{1,0:T(8,128)(2,1)S(1)} %get-tuple-element.18.own_ref), channel_id=1, source_target_pairs={{0,2},{2,0},{1,3},{3,1},{4,6},{6,4},{5,7},{7,5},{8,10},{10,8},{9,1... | collective-permute-start | bytes 786440 | tf_op jit(solution)/shard_map/ppermute | solution.py:266
  77.5 0.0 collective-permute-done.9.y_piece_ref
  77.5 0.7 collective-permute-start.18
  78.2 0.0 collective-permute-done.8.x_piece_ref
  78.2 0.0 collective-permute-start.14
  78.2 4.4 %collective-permute-done.4.y_piece_ref = s16[512,256]{1,0:T(8,128)(2,1)S(1)} collective-permute-done((s16[512,256]{1,0:T(8,128)(2,1)S(1)}, s16[512,256]{1,0:T(8,128)(2,1)S(1)}, u32[]{:S(2)}, u32[]{:S(2)}) %collective-permute-start.4) | collective-permute-done | bytes 262176 | tf_op jit(solution)/shard_map/ppermute | solution.py:267
  82.6 2.0 %collective-permute-start.15 = (s16[512,256]{1,0:T(8,128)(2,1)S(1)}, s16[512,256]{1,0:T(8,128)(2,1)S(1)}, u32[]{:S(2)}, u32[]{:S(2)}) collective-permute-start(s16[512,256]{1,0:T(8,128)(2,1)S(1)} %collective-permute-done.13.x_piece_ref), channel_id=1, source_target_pairs={{0,4},{4,0},{1,5},{5,1},{2,6},{6,2},{3,7},{7,3},{8,12},{12,8},{9,1... | collective-permute-start | bytes 786440 | tf_op jit(solution)/shard_map/ppermute | solution.py:273
  84.7 0.7 collective-permute-start.10
  85.5 4.8 %collective-permute-done.16.x_piece_ref = s16[512,256]{1,0:T(8,128)(2,1)S(1)} collective-permute-done((s16[512,256]{1,0:T(8,128)(2,1)S(1)}, s16[512,256]{1,0:T(8,128)(2,1)S(1)}, u32[]{:S(2)}, u32[]{:S(2)}) %collective-permute-start.16) | collective-permute-done | bytes 262176 | tf_op jit(solution)/shard_map/ppermute | solution.py:266
  90.3 0.0 collective-permute-start.11
  90.3 5.6 %collective-permute-done.18.refs_0_ = s16[512,256]{1,0:T(8,128)(2,1)S(1)} collective-permute-done((s16[512,256]{1,0:T(8,128)(2,1)S(1)}, s16[512,256]{1,0:T(8,128)(2,1)S(1)}, u32[]{:S(2)}, u32[]{:S(2)}) %collective-permute-start.18) | collective-permute-done | bytes 262176 | tf_op jit(solution)/shard_map/ppermute | solution.py:271
  95.9 0.7 collective-permute-start.5
  96.6 0.0 collective-permute-start.6
  96.6 0.6 broadcast_multiply_fusion
  97.1 3.1 %spread.4.refs_1_ = f32[2048,1024]{1,0:T(8,128)} custom-call(s32[7]{0:T(128)S(1)} %stack.31.where_ref, f32[1]{0:T(128)} %get-tuple-element.17.peak_ref, s16[512,256]{1,0:T(8,128)(2,1)S(1)} %get-tuple-element.18.own_ref, s16[512,256]{1,0:T(8,128)(2,1)S(1)} %collective-permute-done.16.x_piece_ref, s16[512,256]{1,0:T(8,128)(2,1)S(1)} %collective-permute-done.17.y_piece_ref, ...), custom_call_target="tpu_custom_call" | custom-call | flops 4194304 | bytes 3145728 | tf_op jit(solution)/shard_map/spread/pallas_call | solution.py:234
  100.2 3.1 %spread.5.refs_2_ = f32[2048,1024]{1,0:T(8,128)} custom-call(s32[7]{0:T(128)S(1)} %stack.31.where_ref, f32[1]{0:T(128)} %get-tuple-element.17.peak_ref, s16[512,256]{1,0:T(8,128)(2,1)S(1)} %collective-permute-done.12.own_ref, s16[512,256]{1,0:T(8,128)(2,1)S(1)} %collective-permute-done.13.x_piece_ref, ...), custom_call_target="tpu_custom_call", output_to_operand_aliasing={{}: (6, {})} | custom-call | flops 4194304 | bytes 3145728 | tf_op jit(solution)/shard_map/spread/pallas_call | solution.py:234
  103.3 3.1 %spread.6.refs_2_ = f32[2048,1024]{1,0:T(8,128)} custom-call(s32[7]{0:T(128)S(1)} %stack.31.where_ref, f32[1]{0:T(128)} %get-tuple-element.17.peak_ref, s16[512,256]{1,0:T(8,128)(2,1)S(1)} %collective-permute-done.7.own_ref, s16[512,256]{1,0:T(8,128)(2,1)S(1)} %collective-permute-done.8.x_piece_ref, ...), custom_call_target="tpu_custom_call", output_to_operand_aliasing={{}: (7, {})} | custom-call | flops 4194304 | bytes 3145728 | tf_op jit(solution)/shard_map/spread/pallas_call | solution.py:234
  106.4 3.1 %spread.7 = f32[2048,1024]{1,0:T(8,128)} custom-call(s32[7]{0:T(128)S(1)} %stack.31.where_ref, f32[1]{0:T(128)} %get-tuple-element.17.peak_ref, s16[512,256]{1,0:T(8,128)(2,1)S(1)} %collective-permute-done.2.own_ref, s16[512,256]{1,0:T(8,128)(2,1)S(1)} %collective-permute-done.3.x_piece_ref, ...), custom_call_target="tpu_custom_call", output_to_operand_aliasing={{}: (7, {})} | custom-call | flops 4194304 | bytes 3145728 | tf_op jit(solution)/shard_map/spread/pallas_call | solution.py:234
  (17 shorter events, 0.1 us)
Async XLA Ops:
  0.6 22.7 %collective-permute-start = (bf16[2048,1024]{1,0:T(8,128)(2,1)}, bf16[2048,1024]{1,0:T(8,128)(2,1)}, u32[]{:S(2)}, u32[]{:S(2)}) collective-permute-start(bf16[2048,1024]{1,0:T(8,128)(2,1)} %param.5), channel_id=1, source_target_pairs={{0,1},{1,0},{2,3},{3,2},{4,5},{5,4},{6,7},{7,6},{8,9},{9,8},{10,11... | collective-permute-start | bytes 12582920 | tf_op jit(solution)/shard_map/ppermute | solution.py:298
  1.2 15.0 %copy-start.1 = (bf16[512,1024]{1,0:T(8,128)(2,1)S(1)}, bf16[512,1024]{1,0:T(8,128)(2,1)}, u32[]{:S(2)}) copy-start(bf16[512,1024]{1,0:T(8,128)(2,1)} %points_ref.1) | copy-start | bytes 3145732
  3.9 33.9 %all-to-all-start = ((bf16[16,272,128]{2,1,0:T(8,128)(2,1)}), bf16[16,272,128]{2,1,0:T(8,128)(2,1)S(1)}, u32[]{:S(2)}, u32[]{:S(2)}) async-start(bf16[16,272,128]{2,1,0:T(8,128)(2,1)} %pack.1), calls=%async_computation | async-start | bytes 2228224 | tf_op jit(solution)/shard_map/all_to_all | solution.py:297
  16.2 4.6 %copy-start = (bf16[2048,1024]{1,0:T(8,128)(2,1)S(1)}, bf16[2048,1024]{1,0:T(8,128)(2,1)}, u32[]{:S(2)}) copy-start(bf16[2048,1024]{1,0:T(8,128)(2,1)} %param.5) | copy-start | bytes 12582916
  37.8 3.3 %collective-permute-start.1 = (bf16[16,272,128]{2,1,0:T(8,128)(2,1)S(1)}, bf16[16,272,128]{2,1,0:T(8,128)(2,1)S(1)}, u32[]{:S(2)}, u32[]{:S(2)}) collective-permute-start(bf16[16,272,128]{2,1,0:T(8,128)(2,1)S(1)} %all-to-all-done.recv_ref), channel_id=1, source_target_pairs={{0,1},{1,0},{2,3},{3,2},{4,5},{5,4},{6,7},{7,6},{8,9},{9,8},{10,11... | collective-permute-start | bytes 3342344 | tf_op jit(solution)/shard_map/ppermute | solution.py:307
  45.6 11.1 %collective-permute-start.12 = (s16[512,256]{1,0:T(8,128)(2,1)S(1)}, s16[512,256]{1,0:T(8,128)(2,1)S(1)}, u32[]{:S(2)}, u32[]{:S(2)}) collective-permute-start(s16[512,256]{1,0:T(8,128)(2,1)S(1)} %get-tuple-element.18.own_ref), channel_id=1, source_target_pairs={{0,8},{8,16},{16,24},{24,0},{1,9},{9,17},{17,25},{25,1},{2,10},{10... | collective-permute-start | bytes 786440 | tf_op jit(solution)/shard_map/ppermute | solution.py:263
  49.2 12.9 %collective-permute-start.7 = (s16[512,256]{1,0:T(8,128)(2,1)S(1)}, s16[512,256]{1,0:T(8,128)(2,1)S(1)}, u32[]{:S(2)}, u32[]{:S(2)}) collective-permute-start(s16[512,256]{1,0:T(8,128)(2,1)S(1)} %get-tuple-element.18.own_ref), channel_id=1, source_target_pairs={{0,24},{8,0},{16,8},{24,16},{1,25},{9,1},{17,9},{25,17},{2,26},{10... | collective-permute-start | bytes 786440 | tf_op jit(solution)/shard_map/ppermute | solution.py:263
  49.7 23.6 %collective-permute-start.2 = (s16[512,256]{1,0:T(8,128)(2,1)S(1)}, s16[512,256]{1,0:T(8,128)(2,1)S(1)}, u32[]{:S(2)}, u32[]{:S(2)}) collective-permute-start(s16[512,256]{1,0:T(8,128)(2,1)S(1)} %get-tuple-element.18.own_ref), channel_id=1, source_target_pairs={{0,16},{8,24},{16,0},{24,8},{1,17},{9,25},{17,1},{25,9},{2,18},{10... | collective-permute-start | bytes 786440 | tf_op jit(solution)/shard_map/ppermute | solution.py:263
  51.3 24.1 %collective-permute-start.17 = (s16[512,256]{1,0:T(8,128)(2,1)S(1)}, s16[512,256]{1,0:T(8,128)(2,1)S(1)}, u32[]{:S(2)}, u32[]{:S(2)}) collective-permute-start(s16[512,256]{1,0:T(8,128)(2,1)S(1)} %get-tuple-element.18.own_ref), channel_id=1, source_target_pairs={{0,4},{4,0},{1,5},{5,1},{2,6},{6,2},{3,7},{7,3},{8,12},{12,8},{9,1... | collective-permute-start | bytes 786440 | tf_op jit(solution)/shard_map/ppermute | solution.py:267
  56.6 19.5 %collective-permute-start.13 = (s16[512,256]{1,0:T(8,128)(2,1)S(1)}, s16[512,256]{1,0:T(8,128)(2,1)S(1)}, u32[]{:S(2)}, u32[]{:S(2)}) collective-permute-start(s16[512,256]{1,0:T(8,128)(2,1)S(1)} %collective-permute-done.12.own_ref), channel_id=1, source_target_pairs={{0,2},{2,0},{1,3},{3,1},{4,6},{6,4},{5,7},{7,5},{8,10},{10,8},{9,1... | collective-permute-start | bytes 786440 | tf_op jit(solution)/shard_map/ppermute | solution.py:266
  62.0 15.5 %collective-permute-start.9 = (s16[512,256]{1,0:T(8,128)(2,1)S(1)}, s16[512,256]{1,0:T(8,128)(2,1)S(1)}, u32[]{:S(2)}, u32[]{:S(2)}) collective-permute-start(s16[512,256]{1,0:T(8,128)(2,1)S(1)} %collective-permute-done.7.own_ref), channel_id=1, source_target_pairs={{0,4},{4,0},{1,5},{5,1},{2,6},{6,2},{3,7},{7,3},{8,12},{12,8},{9,1... | collective-permute-start | bytes 786440 | tf_op jit(solution)/shard_map/ppermute | solution.py:267
  64.2 14.0 %collective-permute-start.8 = (s16[512,256]{1,0:T(8,128)(2,1)S(1)}, s16[512,256]{1,0:T(8,128)(2,1)S(1)}, u32[]{:S(2)}, u32[]{:S(2)}) collective-permute-start(s16[512,256]{1,0:T(8,128)(2,1)S(1)} %collective-permute-done.7.own_ref), channel_id=1, source_target_pairs={{0,2},{2,0},{1,3},{3,1},{4,6},{6,4},{5,7},{7,5},{8,10},{10,8},{9,1... | collective-permute-start | bytes 786440 | tf_op jit(solution)/shard_map/ppermute | solution.py:266
  73.3 9.4 %collective-permute-start.4 = (s16[512,256]{1,0:T(8,128)(2,1)S(1)}, s16[512,256]{1,0:T(8,128)(2,1)S(1)}, u32[]{:S(2)}, u32[]{:S(2)}) collective-permute-start(s16[512,256]{1,0:T(8,128)(2,1)S(1)} %collective-permute-done.2.own_ref), channel_id=1, source_target_pairs={{0,4},{4,0},{1,5},{5,1},{2,6},{6,2},{3,7},{7,3},{8,12},{12,8},{9,1... | collective-permute-start | bytes 786440 | tf_op jit(solution)/shard_map/ppermute | solution.py:267
  75.5 9.2 %collective-permute-start.3 = (s16[512,256]{1,0:T(8,128)(2,1)S(1)}, s16[512,256]{1,0:T(8,128)(2,1)S(1)}, u32[]{:S(2)}, u32[]{:S(2)}) collective-permute-start(s16[512,256]{1,0:T(8,128)(2,1)S(1)} %collective-permute-done.2.own_ref), channel_id=1, source_target_pairs={{0,2},{2,0},{1,3},{3,1},{4,6},{6,4},{5,7},{7,5},{8,10},{10,8},{9,1... | collective-permute-start | bytes 786440 | tf_op jit(solution)/shard_map/ppermute | solution.py:266
  76.2 14.1 %collective-permute-start.16 = (s16[512,256]{1,0:T(8,128)(2,1)S(1)}, s16[512,256]{1,0:T(8,128)(2,1)S(1)}, u32[]{:S(2)}, u32[]{:S(2)}) collective-permute-start(s16[512,256]{1,0:T(8,128)(2,1)S(1)} %get-tuple-element.18.own_ref), channel_id=1, source_target_pairs={{0,2},{2,0},{1,3},{3,1},{4,6},{6,4},{5,7},{7,5},{8,10},{10,8},{9,1... | collective-permute-start | bytes 786440 | tf_op jit(solution)/shard_map/ppermute | solution.py:266
  77.5 18.4 %collective-permute-start.18 = (s16[512,256]{1,0:T(8,128)(2,1)S(1)}, s16[512,256]{1,0:T(8,128)(2,1)S(1)}, u32[]{:S(2)}, u32[]{:S(2)}) collective-permute-start(s16[512,256]{1,0:T(8,128)(2,1)S(1)} %collective-permute-done.17.y_piece_ref), channel_id=1, source_target_pairs={{0,2},{2,0},{1,3},{3,1},{4,6},{6,4},{5,7},{7,5},{8,10},{10,8},{9,1... | collective-permute-start | bytes 786440 | tf_op jit(solution)/shard_map/ppermute | solution.py:271
  78.2 18.4 %collective-permute-start.14 = (s16[512,256]{1,0:T(8,128)(2,1)S(1)}, s16[512,256]{1,0:T(8,128)(2,1)S(1)}, u32[]{:S(2)}, u32[]{:S(2)}) collective-permute-start(s16[512,256]{1,0:T(8,128)(2,1)S(1)} %collective-permute-done.12.own_ref), channel_id=1, source_target_pairs={{0,4},{4,0},{1,5},{5,1},{2,6},{6,2},{3,7},{7,3},{8,12},{12,8},{9,1... | collective-permute-start | bytes 786440 | tf_op jit(solution)/shard_map/ppermute | solution.py:267
  82.6 17.6 %collective-permute-start.15 = (s16[512,256]{1,0:T(8,128)(2,1)S(1)}, s16[512,256]{1,0:T(8,128)(2,1)S(1)}, u32[]{:S(2)}, u32[]{:S(2)}) collective-permute-start(s16[512,256]{1,0:T(8,128)(2,1)S(1)} %collective-permute-done.13.x_piece_ref), channel_id=1, source_target_pairs={{0,4},{4,0},{1,5},{5,1},{2,6},{6,2},{3,7},{7,3},{8,12},{12,8},{9,1... | collective-permute-start | bytes 786440 | tf_op jit(solution)/shard_map/ppermute | solution.py:273
  84.7 18.6 %collective-permute-start.10 = (s16[256,256]{1,0:T(8,128)(2,1)S(1)}, s16[256,256]{1,0:T(8,128)(2,1)S(1)}, u32[]{:S(2)}, u32[]{:S(2)}) collective-permute-start(s16[256,256]{1,0:T(8,128)(2,1)S(1)} %slice.18), channel_id=1, source_target_pairs={{0,2},{2,0},{1,3},{3,1},{4,6},{6,4},{5,7},{7,5},{8,10},{10,8},{9,1... | collective-permute-start | bytes 393224 | tf_op jit(solution)/shard_map/ppermute | solution.py:271
  90.3 13.0 %collective-permute-start.11 = (s16[256,256]{1,0:T(8,128)(2,1)S(1)}, s16[256,256]{1,0:T(8,128)(2,1)S(1)}, u32[]{:S(2)}, u32[]{:S(2)}) collective-permute-start(s16[256,256]{1,0:T(8,128)(2,1)S(1)} %slice.19), channel_id=1, source_target_pairs={{0,4},{4,0},{1,5},{5,1},{2,6},{6,2},{3,7},{7,3},{8,12},{12,8},{9,1... | collective-permute-start | bytes 393224 | tf_op jit(solution)/shard_map/ppermute | solution.py:273
  95.9 10.5 %collective-permute-start.5 = (s16[256,256]{1,0:T(8,128)(2,1)S(1)}, s16[256,256]{1,0:T(8,128)(2,1)S(1)}, u32[]{:S(2)}, u32[]{:S(2)}) collective-permute-start(s16[256,256]{1,0:T(8,128)(2,1)S(1)} %slice.16), channel_id=1, source_target_pairs={{0,2},{2,0},{1,3},{3,1},{4,6},{6,4},{5,7},{7,5},{8,10},{10,8},{9,1... | collective-permute-start | bytes 393224 | tf_op jit(solution)/shard_map/ppermute | solution.py:271
  96.6 9.8 %collective-permute-start.6 = (s16[256,256]{1,0:T(8,128)(2,1)S(1)}, s16[256,256]{1,0:T(8,128)(2,1)S(1)}, u32[]{:S(2)}, u32[]{:S(2)}) collective-permute-start(s16[256,256]{1,0:T(8,128)(2,1)S(1)} %slice.17), channel_id=1, source_target_pairs={{0,4},{4,0},{1,5},{5,1},{2,6},{6,2},{3,7},{7,3},{8,12},{12,8},{9,1... | collective-permute-start | bytes 393224 | tf_op jit(solution)/shard_map/ppermute | solution.py:273
where the time goes:
time: 110 us; the launch traced here: 109 us
  waiting for transfers between devices  38.8 us (35%)
  starting transfers between devices  27.2 us (25%)
  Pallas kernels  22.7 us (21%)
  other arithmetic  10.7 us (10%)
  matrix products  7.2 us (7%)
  local copies, waits for them, and re-layouts  1.37 us (1%)
  between operations  1.36 us (1%)
    ppermute x3, waiting for transfers between devices, gather(): held.append(lax.ppermute(unit, 'z', [(i, (i + s) % nz) for i in range(nz)]))  17.3 us
    pallas_call x4, Pallas kernels, spread(): pl.pallas_call(functools.partial(spread_kernel, len(diagonal)), grid_spec...  12.3 us
    all_to_all x1, starting transfers between devices, shards(): recv = lax.all_to_all(parcels, OWNERS, 0, 0, tiled=True)  7.87 us
    dot_general x2, matrix products, nearest(): lax.dot_general(points, part, (((1,), (1,)), ((), ())), preferred_element...  7.2 us
    all_to_all x1, waiting for transfers between devices, shards(): recv = lax.all_to_all(parcels, OWNERS, 0, 0, tiled=True)  6.71 us
    reduce_sum x2, other arithmetic, nearest(): part_sq = jnp.sum(part_f * part_f, axis=1)  6.15 us
    ppermute x3, starting transfers between devices, gather(): held.append(lax.ppermute(unit, 'z', [(i, (i + s) % nz) for i in range(nz)]))  5.75 us
    ppermute x3, waiting for transfers between devices, gather(): diagonal.append(lax.ppermute(from_y[:cut], 'x', SWAP))  5.62 us
  transfers between devices with their start and end apart: 20, of which 7 were waited for; matrix products, arithmetic and copies ran while one was open for 18% of the time, Pallas kernels for 14%

commit v1 on v0

--- a/solution.py
+++ b/solution.py
@@ -23,6 +23,7 @@
 OWNERS = ("z", "y", "x")
 AXES = ("g",) + OWNERS + ("mp",)
 
+SPREADS = ((0, 2), (2, 5), (5, 8))
 VMEM = pl.BlockSpec(memory_space=pltpu.VMEM)
 SMEM = pl.BlockSpec(memory_space=pltpu.SMEM)
 
@@ -197,54 +198,56 @@
     )(where, peak, acc, prior)
 
 
-def spread_kernel(parts, where_ref, peak_ref, own_ref, x_piece_ref, y_piece_ref, *refs):
+def spread_kernel(counts, where_ref, peak_ref, *refs):
     out_ref = refs[-1]
-    high_size = own_ref.shape[0]
     first = where_ref[1] == 0
-    y = where_ref[2]
-
-    def emit(mine_ref, at, other_ref, column):
-        rows = other_ref.shape[0]
-        lower = lax.broadcasted_iota(jnp.int16, (rows, LANES), 1) < HALF
-        lanes = pl.ds(pl.multiple_of(column * LANES, LANES), LANES)
-        mine, other = mine_ref[at : at + rows, :], other_ref[...]
-        left, right = jnp.where(first, mine, other), jnp.where(first, other, mine)
-        both = (
-            jnp.where(lower, left, pltpu.roll(right, HALF, 1)),
-            jnp.where(lower, pltpu.roll(left, HALF, 1), right),
-        )
-        for k, level in enumerate(both):
-            t = level.astype(I32).astype(F32) * (1.0 / LEVELS)
-            s = t * jnp.abs(t)
-            start = k * high_size + at
-            out_ref[start : start + rows, lanes] = s * jnp.abs(s) * peak_ref[0]
-
-    emit(own_ref, 0, x_piece_ref, y)
+    high_size = out_ref.shape[0] // LOW
+
+    def emit(mine_ref, other_refs):
+        at = 0
+        for other_ref in other_refs:
+            rows = other_ref.shape[0]
+            lower = lax.broadcasted_iota(jnp.int16, (rows, LANES), 1) < HALF
+            for l in range(0, LOW, 2):
+                lanes = slice(l * COLS, (l + 2) * COLS)
+                mine, other = mine_ref[at : at + rows, lanes], other_ref[:, lanes]
+                left, right = jnp.where(first, mine, other), jnp.where(first, other, mine)
+                both = (
+                    jnp.where(lower, left, pltpu.roll(right, HALF, 1)),
+                    jnp.where(lower, pltpu.roll(left, HALF, 1), right),
+                )
+                for k, level in enumerate(both):
+                    t = level.astype(I32).astype(F32) * (1.0 / LEVELS)
+                    s = t * jnp.abs(t)
+                    start = (l + k) * high_size + at
+                    out_ref[start : start + rows, :] = s * jnp.abs(s) * peak_ref[0]
+            at += rows
+
     at = 0
-    for ref in refs[:parts]:
-        emit(y_piece_ref, at, ref, 1 - y)
-        at += ref.shape[0]
-
-
-def spread(n, own, x_piece, y_piece, diagonal, where, peak, width, into):
-    high_size, _ = own.shape
+    for p, count in enumerate(counts):
+        pl.when(pl.program_id(0) == p)(functools.partial(emit, refs[at], refs[at + 1 : at + 1 + count]))
+        at += 1 + count
+
+
+def spread(first, pairs, where, peak, width, into):
+    high_size = pairs[0][0].shape[0]
     total = LOW * high_size
-    pieces = [own, x_piece, y_piece, *diagonal]
+    pieces = [p for mine, others in pairs for p in (mine, *others)]
     extra = [] if into is None else [into]
     return pl.pallas_call(
-        functools.partial(spread_kernel, len(diagonal)),
+        functools.partial(spread_kernel, tuple(len(others) for _, others in pairs)),
         grid_spec=pltpu.PrefetchScalarGridSpec(
             num_scalar_prefetch=1,
-            grid=(LOW // 2,),
-            in_specs=[SMEM]
-            + [pl.BlockSpec((p.shape[0], LANES), lambda i, w: (0, i)) for p in pieces]
-            + [pl.BlockSpec(memory_space=pl.ANY) for _ in extra],
-            out_specs=pl.BlockSpec((2 * high_size, 2 * LANES), lambda i, w: (i, w[3 + n])),
+            grid=(len(pairs),),
+            in_specs=[SMEM] + [VMEM for _ in pieces] + [pl.BlockSpec(memory_space=pl.ANY) for _ in extra],
+            out_specs=pl.BlockSpec((total, LANES), lambda p, w: (0, w[2 + first + p])),
         ),
         out_shape=jax.ShapeDtypeStruct((total, width), F32),
         input_output_aliases={2 + len(pieces): 0} if extra else {},
         cost_estimate=pl.CostEstimate(
-            flops=16 * total * LANES, bytes_accessed=12 * total * LANES, transcendentals=0
+            flops=8 * len(pairs) * total * LANES,
+            bytes_accessed=6 * len(pairs) * total * LANES,
+            transcendentals=0,
         ),
         compiler_params=pltpu.CompilerParams(vmem_limit_bytes=SMALL_VMEM),
         name="spread",
@@ -257,21 +260,30 @@
 
 def gather(unit, peak, where, width):
     nz = lax.axis_size("z")
-    rows = unit.shape[0]
-    held = [unit]
-    for n, s in enumerate(z_shifts(nz)[1:], 1):
-        held.append(lax.ppermute(unit, "z", [(i, (i + s) % nz) for i in range(nz)]))
+    assert nz == 4
+    half = unit.shape[0] // 2
+
+    def send(piece, axis, shift=1):
+        size = lax.axis_size(axis)
+        return lax.ppermute(piece, axis, [(i, (i + shift) % size) for i in range(size)])
+
+    shifts = z_shifts(nz)
+    held = [unit] + [send(unit, "z", shifts[n]) for n in range(1, nz)]
+    from_x = [send(piece, "x") for piece in held]
+    from_y = [send(piece, "y") for piece in held]
+    near = send(from_y[0], "x")
+    diagonal = [
+        [near],
+        [send(from_x[1], "y")],
+        [send(from_y[2][:half], "x"), send(from_x[2][half:], "y")],
+        [send(near, "z", shifts[3])],
+    ]
+    pairs = []
+    for n in range(nz):
+        pairs += [(held[n], [from_x[n]]), (from_y[n], diagonal[n])]
     out = None
-    for n, piece in enumerate(held):
-        from_x = lax.ppermute(piece, "x", SWAP)
-        from_y = lax.ppermute(piece, "y", SWAP)
-        cut = (rows, 0)[n] if n < 2 else rows // 2
-        diagonal = []
-        if cut:
-            diagonal.append(lax.ppermute(from_y[:cut], "x", SWAP))
-        if cut < rows:
-            diagonal.append(lax.ppermute(from_x[cut:], "y", SWAP))
-        out = spread(n, piece, from_x, from_y, diagonal, where, peak, width, out)
+    for start, end in SPREADS:
+        out = spread(start, pairs[start:end], where, peak, width, out)
     return out
 
 
@@ -290,8 +302,8 @@
     nz, ny, nx = (lax.axis_size(a) for a in OWNERS)
     assert nx == 2 and ny == 2 and nz * ny * nx * COLS == width
     block = z * ny + y
-    blocks = [(z - s) % nz for s in z_shifts(nz)]
-    where = jnp.stack([lax.axis_index("mp") * shard_rows, x, y, *blocks]).astype(I32)
+    columns = [((z - s) % nz) * ny + (y ^ m) for s in z_shifts(nz) for m in range(ny)]
+    where = jnp.stack([lax.axis_index("mp") * shard_rows, x, *columns]).astype(I32)
 
     parcels = pack(points, assign, keep_mask)
     recv = lax.all_to_all(parcels, OWNERS, 0, 0, tiled=True)

time: 110 us -> 102 us (0.927)
  waiting for transfers between devices: 38.8 us -> 23.6 us
  starting transfers between devices: 27.2 us -> 35.9 us
  Pallas kernels: 22.7 us -> 21.4 us
    ppermute x17 -> x16, waiting for transfers between devices: 32.1 us -> 17.1 us  [send(): lax.ppermute(piece, axis, [(i, (i + shift) % size) for i in range(size)])]
    ppermute x17 -> x16, starting transfers between devices: 18.8 us -> 27.5 us  [send(): lax.ppermute(piece, axis, [(i, (i + shift) % size) for i in range(size)])]
    pallas_call x4 -> x3, Pallas kernels: 12.3 us -> 10.9 us  [spread(): pl.pallas_call(functools.partial(spread_kernel, tuple((len(others) for _,...]
  transfers between devices with their start and end apart: 20 -> 19, of which waited for: 7 -> 7; matrix products, arithmetic and copies ran while one was open for 18% -> 19% of each run, Pallas kernels for 14% -> 13%
where the time goes in v1:
time: 102 us
  starting transfers between devices  35.9 us (35%)
  waiting for transfers between devices  23.6 us (23%)
  Pallas kernels  21.4 us (21%)
  other arithmetic  10.9 us (11%)
  matrix products  7.2 us (7%)
  between operations  1.52 us (1%)
  local copies, waits for them, and re-layouts  1.35 us (1%)
    ppermute x16, starting transfers between devices, send(): lax.ppermute(piece, axis, [(i, (i + shift) % size) for i in range(size)])  27.5 us
    ppermute x16, waiting for transfers between devices, send(): lax.ppermute(piece, axis, [(i, (i + shift) % size) for i in range(size)])  17.1 us
    pallas_call x3, Pallas kernels, spread(): pl.pallas_call(functools.partial(spread_kernel, tuple((len(others) for _,...  10.9 us
    all_to_all x1, starting transfers between devices, shards(): recv = lax.all_to_all(parcels, OWNERS, 0, 0, tiled=True)  7.87 us
    dot_general x2, matrix products, nearest(): lax.dot_general(points, part, (((1,), (1,)), ((), ())), preferred_element...  7.2 us
    all_to_all x1, waiting for transfers between devices, shards(): recv = lax.all_to_all(parcels, OWNERS, 0, 0, tiled=True)  6.44 us
    reduce_sum x2, other arithmetic, nearest(): part_sq = jnp.sum(part_f * part_f, axis=1)  6.15 us
    pallas_call x1, Pallas kernels, last_sums(): pl.pallas_call(last_kernel, out_shape=(unit_shape(high_size), jax.ShapeDt...  4.45 us
  transfers between devices with their start and end apart: 19, of which 7 were waited for; matrix products, arithmetic and copies ran while one was open for 19% of the time, Pallas kernels for 13%

profile of v1, /device:TPU:0, one launch (start us, length us, event | category | flops | bytes accessed | tf_op | source)
XLA Modules:
  0.0 101.8 jit_solution(3226988640094003807)
XLA Ops:
  0.6 0.6 collective-permute-start
  1.2 2.7 %pack.1 = bf16[16,272,128]{2,1,0:T(8,128)(2,1)} custom-call(bf16[512,1024]{1,0:T(8,128)(2,1)} %points_ref.1, s32[4,128]{1,0:T(4,128)} %bitcast.17, s32[4,128]{1,0:T(4,128)} %bitcast.18), custom_call_target="tpu_custom_call" | custom-call | flops 1048576 | bytes 2097152 | tf_op jit(solution)/shard_map/pack/pallas_call | solution.py:58
  3.9 7.9 %all-to-all-start = ((bf16[16,272,128]{2,1,0:T(8,128)(2,1)}), bf16[16,272,128]{2,1,0:T(8,128)(2,1)S(1)}, u32[]{:S(2)}, u32[]{:S(2)}) async-start(bf16[16,272,128]{2,1,0:T(8,128)(2,1)} %pack.1), calls=%async_computation | async-start | bytes 2228224 | tf_op jit(solution)/shard_map/all_to_all | solution.py:309
  11.8 3.8 %abs_reduce_fusion = bf16[]{:T(256)} fusion(bf16[2048,1024]{1,0:T(8,128)(2,1)} %param.5), kind=kLoop, calls=%fused_computation.2 | loop fusion | flops 4194303 | bytes 4194306 | tf_op jit(solution)/shard_map/reduce_max | solution.py:315
  16.3 0.1 stack.43.where_ref
  16.4 0.0 copy-start
  16.5 0.3 multiply_reduce_fusion.2
  16.7 1.2 %constant_dynamic-slice_fusion.prior_ref = bf16[2048,128]{1,0:T(8,128)(2,1)S(1)} fusion(bf16[2048,1024]{1,0:T(8,128)(2,1)} %param.5, s32[]{:T(128)S(6)} %select_n.30), kind=kLoop, calls=%fused_computation.7 | loop fusion | bytes 1048580 | tf_op jit(solution)/shard_map/dynamic_slice | solution.py:316
  18.0 3.1 %multiply_reduce_fusion.1 = f32[2048]{0:T(1024)S(1)} fusion(bf16[2048,1024]{1,0:T(8,128)(2,1)} %param.5), kind=kLoop, calls=%fused_computation.1 | loop fusion | flops 6289408 | bytes 4202496 | tf_op jit(solution)/shard_map/reduce_sum | solution.py:293
  21.1 2.5 %add_reduce_fusion.1 = f32[512]{0:T(512)S(1)} fusion(bf16[512,1024]{1,0:T(8,128)(2,1)S(1)} %copy-done.1, bf16[2048,1024]{1,0:T(8,128)(2,1)S(1)} %copy-done, f32[2048]{0:T(1024)S(1)} %multiply_reduce_fusion.1, f32[512]{0:T(512)S(1)} %multiply_reduce_fusion.2), kind=kOutput, calls=%fused_computation.4 | convolution fusion | flops 2151677440 | bytes 5255168 | tf_op jit(solution)/shard_map/dot_general | solution.py:291
  23.6 3.1 %multiply_reduce_fusion = f32[2048]{0:T(1024)S(1)} fusion(bf16[2048,1024]{1,0:T(8,128)(2,1)} %collective-permute-done), kind=kLoop, calls=%fused_computation | loop fusion | flops 6289408 | bytes 4202496 | tf_op jit(solution)/shard_map/reduce_sum | solution.py:293
  26.7 4.7 %add_reduce_fusion = f32[512]{0:T(512)S(1)} fusion(f32[2048]{0:T(1024)S(1)} %multiply_reduce_fusion, f32[512]{0:T(512)S(1)} %multiply_reduce_fusion.2, bf16[512,1024]{1,0:T(8,128)(2,1)S(1)} %copy-done.1, bf16[2048,1024]{1,0:T(8,128)(2,1)} %collective-permute-done), kind=kOutput, calls=%fused_computation.3 | convolution fusion | flops 2151677440 | bytes 5255168 | tf_op jit(solution)/shard_map/dot_general | solution.py:291
  31.4 6.4 %all-to-all-done.recv_ref = bf16[16,272,128]{2,1,0:T(8,128)(2,1)S(1)} async-done(((bf16[16,272,128]{2,1,0:T(8,128)(2,1)}), bf16[16,272,128]{2,1,0:T(8,128)(2,1)S(1)}, u32[]{:S(2)}, u32[]{:S(2)}) %all-to-all-start) | async-done | bytes 1114144 | tf_op jit(solution)/shard_map/all_to_all | solution.py:309
  37.8 3.3 %sums_first.1 = (f32[272,512]{1,0:T(8,128)S(1)}, f32[8,128]{1,0:T(8,128)S(1)}) custom-call(s32[10]{0:T(128)S(1)} %stack.43.where_ref, bf16[16,272,128]{2,1,0:T(8,128)(2,1)S(1)} %all-to-all-done.recv_ref), custom_call_target="tpu_custom_call" | custom-call | flops 2281701376 | bytes 1114112 | tf_op jit(solution)/shard_map/sums_first/pallas_call | solution.py:163
  41.1 0.0 collective-permute-done.1.recv_ref
  41.1 4.5 %sums_last.1 = (s16[512,256]{1,0:T(8,128)(2,1)S(1)}, f32[1]{0:T(128)}) custom-call(s32[10]{0:T(128)S(1)} %stack.43.where_ref, f32[1]{0:T(128)} %bitcast.2.least_ref, bf16[16,272,128]{2,1,0:T(8,128)(2,1)S(1)} %collective-permute-done.1.recv_ref, f32[272,512]{1,0:T(8,128)S(1)} %get-tuple-element.14.given_ref, f32[8,128]{1,0:T(8,128)S(1)} %get-tuple-element.15.given_peak_ref, ...), custom_call_target="tpu_custom_call" | custom-call | flops 2281701376 | bytes 1114112 | tf_op jit(solution)/shard_map/sums_last/pallas_call | solution.py:179
  45.6 3.6 %collective-permute-start.13 = (s16[512,256]{1,0:T(8,128)(2,1)S(1)}, s16[512,256]{1,0:T(8,128)(2,1)S(1)}, u32[]{:S(2)}, u32[]{:S(2)}) collective-permute-start(s16[512,256]{1,0:T(8,128)(2,1)S(1)} %get-tuple-element.18.refs_0_), channel_id=1, source_target_pairs={{0,8},{8,16},{16,24},{24,0},{1,9},{9,17},{17,25},{25,1},{2,10},{10... | collective-permute-start | bytes 786440 | tf_op jit(solution)/shard_map/ppermute | solution.py:268
  49.2 1.3 %collective-permute-start.10 = (s16[512,256]{1,0:T(8,128)(2,1)S(1)}, s16[512,256]{1,0:T(8,128)(2,1)S(1)}, u32[]{:S(2)}, u32[]{:S(2)}) collective-permute-start(s16[512,256]{1,0:T(8,128)(2,1)S(1)} %get-tuple-element.18.refs_0_), channel_id=1, source_target_pairs={{0,4},{4,0},{1,5},{5,1},{2,6},{6,2},{3,7},{7,3},{8,12},{12,8},{9,1... | collective-permute-start | bytes 786440 | tf_op jit(solution)/shard_map/ppermute | solution.py:268
  50.5 1.2 %collective-permute-start.2 = (s16[512,256]{1,0:T(8,128)(2,1)S(1)}, s16[512,256]{1,0:T(8,128)(2,1)S(1)}, u32[]{:S(2)}, u32[]{:S(2)}) collective-permute-start(s16[512,256]{1,0:T(8,128)(2,1)S(1)} %get-tuple-element.18.refs_0_), channel_id=1, source_target_pairs={{0,24},{8,0},{16,8},{24,16},{1,25},{9,1},{17,9},{25,17},{2,26},{10... | collective-permute-start | bytes 786440 | tf_op jit(solution)/shard_map/ppermute | solution.py:268
  51.7 0.7 collective-permute-start.17
  52.4 0.5 collective-permute-start.7
  52.9 3.7 %collective-permute-done.13.refs_0_ = s16[512,256]{1,0:T(8,128)(2,1)S(1)} collective-permute-done((s16[512,256]{1,0:T(8,128)(2,1)S(1)}, s16[512,256]{1,0:T(8,128)(2,1)S(1)}, u32[]{:S(2)}, u32[]{:S(2)}) %collective-permute-start.13) | collective-permute-done | bytes 262176 | tf_op jit(solution)/shard_map/ppermute | solution.py:268
  56.6 0.9 collective-permute-start.14
  57.5 0.1 collective-permute-done.10.refs_2_
  57.6 1.1 %collective-permute-start.11 = (s16[512,256]{1,0:T(8,128)(2,1)S(1)}, s16[512,256]{1,0:T(8,128)(2,1)S(1)}, u32[]{:S(2)}, u32[]{:S(2)}) collective-permute-start(s16[512,256]{1,0:T(8,128)(2,1)S(1)} %collective-permute-done.10.refs_2_), channel_id=1, source_target_pairs={{0,2},{2,0},{1,3},{3,1},{4,6},{6,4},{5,7},{7,5},{8,10},{10,8},{9,1... | collective-permute-start | bytes 786440 | tf_op jit(solution)/shard_map/ppermute | solution.py:268
  58.7 3.3 %collective-permute-done.2.refs_4_ = s16[512,256]{1,0:T(8,128)(2,1)S(1)} collective-permute-done((s16[512,256]{1,0:T(8,128)(2,1)S(1)}, s16[512,256]{1,0:T(8,128)(2,1)S(1)}, u32[]{:S(2)}, u32[]{:S(2)}) %collective-permute-start.2) | collective-permute-done | bytes 262176 | tf_op jit(solution)/shard_map/ppermute | solution.py:268
  62.0 0.7 collective-permute-start.5
  62.7 0.0 collective-permute-done.17.refs_1_
  62.7 2.2 %collective-permute-start.3 = (s16[512,256]{1,0:T(8,128)(2,1)S(1)}, s16[512,256]{1,0:T(8,128)(2,1)S(1)}, u32[]{:S(2)}, u32[]{:S(2)}) collective-permute-start(s16[512,256]{1,0:T(8,128)(2,1)S(1)} %collective-permute-done.2.refs_4_), channel_id=1, source_target_pairs={{0,4},{4,0},{1,5},{5,1},{2,6},{6,2},{3,7},{7,3},{8,12},{12,8},{9,1... | collective-permute-start | bytes 786440 | tf_op jit(solution)/shard_map/ppermute | solution.py:268
  64.9 8.3 %collective-permute-done.7.refs_3_ = s16[512,256]{1,0:T(8,128)(2,1)S(1)} collective-permute-done((s16[512,256]{1,0:T(8,128)(2,1)S(1)}, s16[512,256]{1,0:T(8,128)(2,1)S(1)}, u32[]{:S(2)}, u32[]{:S(2)}) %collective-permute-start.7) | collective-permute-done | bytes 262176 | tf_op jit(solution)/shard_map/ppermute | solution.py:268
  73.3 2.2 %collective-permute-start.15 = (s16[512,256]{1,0:T(8,128)(2,1)S(1)}, s16[512,256]{1,0:T(8,128)(2,1)S(1)}, u32[]{:S(2)}, u32[]{:S(2)}) collective-permute-start(s16[512,256]{1,0:T(8,128)(2,1)S(1)} %collective-permute-done.13.refs_0_), channel_id=1, source_target_pairs={{0,4},{4,0},{1,5},{5,1},{2,6},{6,2},{3,7},{7,3},{8,12},{12,8},{9,1... | collective-permute-start | bytes 786440 | tf_op jit(solution)/shard_map/ppermute | solution.py:268
  75.5 0.0 collective-permute-done.14.refs_1_
  75.5 0.0 collective-permute-start.16
  75.5 0.0 collective-permute-done.11.refs_3_
  75.5 0.7 collective-permute-start.8
  76.2 0.5 collective-permute-done.5.refs_5_
  76.7 1.5 %collective-permute-start.9 = (s16[512,256]{1,0:T(8,128)(2,1)S(1)}, s16[512,256]{1,0:T(8,128)(2,1)S(1)}, u32[]{:S(2)}, u32[]{:S(2)}) collective-permute-start(s16[512,256]{1,0:T(8,128)(2,1)S(1)} %collective-permute-done.7.refs_3_), channel_id=1, source_target_pairs={{0,4},{4,0},{1,5},{5,1},{2,6},{6,2},{3,7},{7,3},{8,12},{12,8},{9,1... | collective-permute-start | bytes 786440 | tf_op jit(solution)/shard_map/ppermute | solution.py:268
  78.2 0.0 collective-permute-done.3.refs_0_
  78.2 6.3 %collective-permute-start.12 = (s16[512,256]{1,0:T(8,128)(2,1)S(1)}, s16[512,256]{1,0:T(8,128)(2,1)S(1)}, u32[]{:S(2)}, u32[]{:S(2)}) collective-permute-start(s16[512,256]{1,0:T(8,128)(2,1)S(1)} %collective-permute-done.11.refs_3_), channel_id=1, source_target_pairs={{0,16},{8,24},{16,0},{24,8},{1,17},{9,25},{17,1},{25,9},{2,18},{10... | collective-permute-start | bytes 786440 | tf_op jit(solution)/shard_map/ppermute | solution.py:268
  84.6 2.5 %collective-permute-start.4 = (s16[256,256]{1,0:T(8,128)(2,1)S(1)}, s16[256,256]{1,0:T(8,128)(2,1)S(1)}, u32[]{:S(2)}, u32[]{:S(2)}) collective-permute-start(s16[256,256]{1,0:T(8,128)(2,1)S(1)} %slice.8), channel_id=1, source_target_pairs={{0,2},{2,0},{1,3},{3,1},{4,6},{6,4},{5,7},{7,5},{8,10},{10,8},{9,1... | collective-permute-start | bytes 393224 | tf_op jit(solution)/shard_map/ppermute | solution.py:268
  87.1 1.1 %collective-permute-done.16.refs_3_ = s16[512,256]{1,0:T(8,128)(2,1)S(1)} collective-permute-done((s16[512,256]{1,0:T(8,128)(2,1)S(1)}, s16[512,256]{1,0:T(8,128)(2,1)S(1)}, u32[]{:S(2)}, u32[]{:S(2)}) %collective-permute-start.16) | collective-permute-done | bytes 262176 | tf_op jit(solution)/shard_map/ppermute | solution.py:268
  88.2 2.0 %collective-permute-start.6 = (s16[256,256]{1,0:T(8,128)(2,1)S(1)}, s16[256,256]{1,0:T(8,128)(2,1)S(1)}, u32[]{:S(2)}, u32[]{:S(2)}) collective-permute-start(s16[256,256]{1,0:T(8,128)(2,1)S(1)} %slice.9), channel_id=1, source_target_pairs={{0,4},{4,0},{1,5},{5,1},{2,6},{6,2},{3,7},{7,3},{8,12},{12,8},{9,1... | collective-permute-start | bytes 393224 | tf_op jit(solution)/shard_map/ppermute | solution.py:268
  90.3 0.6 broadcast_multiply_fusion
  90.8 3.0 %spread.3.refs_6_ = f32[2048,1024]{1,0:T(8,128)} custom-call(s32[10]{0:T(128)S(1)} %stack.43.where_ref, f32[1]{0:T(128)} %get-tuple-element.17.peak_ref, s16[512,256]{1,0:T(8,128)(2,1)S(1)} %get-tuple-element.18.refs_0_, s16[512,256]{1,0:T(8,128)(2,1)S(1)} %collective-permute-done.17.refs_1_, s16[512,256]{1,0:T(8,128)(2,1)S(1)} %collective-permute-done.10.refs_2_, ...), custom_call_target="tpu_custom_call" | custom-call | flops 4194304 | bytes 3145728 | tf_op jit(solution)/shard_map/spread/pallas_call | solution.py:237
  93.8 4.0 %spread.4.refs_7_ = f32[2048,1024]{1,0:T(8,128)} custom-call(s32[10]{0:T(128)S(1)} %stack.43.where_ref, f32[1]{0:T(128)} %get-tuple-element.17.peak_ref, s16[512,256]{1,0:T(8,128)(2,1)S(1)} %collective-permute-done.13.refs_0_, s16[512,256]{1,0:T(8,128)(2,1)S(1)} %collective-permute-done.14.refs_1_, ...), custom_call_target="tpu_custom_call", output_to_operand_aliasing={{}: (8, {})} | custom-call | flops 6291456 | bytes 4718592 | tf_op jit(solution)/shard_map/spread/pallas_call | solution.py:237
  97.8 0.0 collective-permute-done.6.refs_2_
  97.8 0.0 collective-permute-done.12.refs_6_
  97.8 4.0 %spread.5 = f32[2048,1024]{1,0:T(8,128)} custom-call(s32[10]{0:T(128)S(1)} %stack.43.where_ref, f32[1]{0:T(128)} %get-tuple-element.17.peak_ref, s16[512,256]{1,0:T(8,128)(2,1)S(1)} %collective-permute-done.3.refs_0_, s16[256,256]{1,0:T(8,128)(2,1)S(1)} %collective-permute-done.4.refs_1_, ...), custom_call_target="tpu_custom_call", output_to_operand_aliasing={{}: (9, {})} | custom-call | flops 6291456 | bytes 4718592 | tf_op jit(solution)/shard_map/spread/pallas_call | solution.py:237
  (12 shorter events, 0.0 us)
Async XLA Ops:
  0.6 23.0 %collective-permute-start = (bf16[2048,1024]{1,0:T(8,128)(2,1)}, bf16[2048,1024]{1,0:T(8,128)(2,1)}, u32[]{:S(2)}, u32[]{:S(2)}) collective-permute-start(bf16[2048,1024]{1,0:T(8,128)(2,1)} %param.5), channel_id=1, source_target_pairs={{0,1},{1,0},{2,3},{3,2},{4,5},{5,4},{6,7},{7,6},{8,9},{9,8},{10,11... | collective-permute-start | bytes 12582920 | tf_op jit(solution)/shard_map/ppermute | solution.py:310
  1.2 15.3 %copy-start.1 = (bf16[512,1024]{1,0:T(8,128)(2,1)S(1)}, bf16[512,1024]{1,0:T(8,128)(2,1)}, u32[]{:S(2)}) copy-start(bf16[512,1024]{1,0:T(8,128)(2,1)} %points_ref.1) | copy-start | bytes 3145732
  3.9 33.9 %all-to-all-start = ((bf16[16,272,128]{2,1,0:T(8,128)(2,1)}), bf16[16,272,128]{2,1,0:T(8,128)(2,1)S(1)}, u32[]{:S(2)}, u32[]{:S(2)}) async-start(bf16[16,272,128]{2,1,0:T(8,128)(2,1)} %pack.1), calls=%async_computation | async-start | bytes 2228224 | tf_op jit(solution)/shard_map/all_to_all | solution.py:309
  16.4 4.6 %copy-start = (bf16[2048,1024]{1,0:T(8,128)(2,1)S(1)}, bf16[2048,1024]{1,0:T(8,128)(2,1)}, u32[]{:S(2)}) copy-start(bf16[2048,1024]{1,0:T(8,128)(2,1)} %param.5) | copy-start | bytes 12582916
  37.8 3.3 %collective-permute-start.1 = (bf16[16,272,128]{2,1,0:T(8,128)(2,1)S(1)}, bf16[16,272,128]{2,1,0:T(8,128)(2,1)S(1)}, u32[]{:S(2)}, u32[]{:S(2)}) collective-permute-start(bf16[16,272,128]{2,1,0:T(8,128)(2,1)S(1)} %all-to-all-done.recv_ref), channel_id=1, source_target_pairs={{0,1},{1,0},{2,3},{3,2},{4,5},{5,4},{6,7},{7,6},{8,9},{9,8},{10,11... | collective-permute-start | bytes 3342344 | tf_op jit(solution)/shard_map/ppermute | solution.py:319
  45.6 11.1 %collective-permute-start.13 = (s16[512,256]{1,0:T(8,128)(2,1)S(1)}, s16[512,256]{1,0:T(8,128)(2,1)S(1)}, u32[]{:S(2)}, u32[]{:S(2)}) collective-permute-start(s16[512,256]{1,0:T(8,128)(2,1)S(1)} %get-tuple-element.18.refs_0_), channel_id=1, source_target_pairs={{0,8},{8,16},{16,24},{24,0},{1,9},{9,17},{17,25},{25,1},{2,10},{10... | collective-permute-start | bytes 786440 | tf_op jit(solution)/shard_map/ppermute | solution.py:268
  49.2 8.4 %collective-permute-start.10 = (s16[512,256]{1,0:T(8,128)(2,1)S(1)}, s16[512,256]{1,0:T(8,128)(2,1)S(1)}, u32[]{:S(2)}, u32[]{:S(2)}) collective-permute-start(s16[512,256]{1,0:T(8,128)(2,1)S(1)} %get-tuple-element.18.refs_0_), channel_id=1, source_target_pairs={{0,4},{4,0},{1,5},{5,1},{2,6},{6,2},{3,7},{7,3},{8,12},{12,8},{9,1... | collective-permute-start | bytes 786440 | tf_op jit(solution)/shard_map/ppermute | solution.py:268
  50.5 11.5 %collective-permute-start.2 = (s16[512,256]{1,0:T(8,128)(2,1)S(1)}, s16[512,256]{1,0:T(8,128)(2,1)S(1)}, u32[]{:S(2)}, u32[]{:S(2)}) collective-permute-start(s16[512,256]{1,0:T(8,128)(2,1)S(1)} %get-tuple-element.18.refs_0_), channel_id=1, source_target_pairs={{0,24},{8,0},{16,8},{24,16},{1,25},{9,1},{17,9},{25,17},{2,26},{10... | collective-permute-start | bytes 786440 | tf_op jit(solution)/shard_map/ppermute | solution.py:268
  51.7 11.0 %collective-permute-start.17 = (s16[512,256]{1,0:T(8,128)(2,1)S(1)}, s16[512,256]{1,0:T(8,128)(2,1)S(1)}, u32[]{:S(2)}, u32[]{:S(2)}) collective-permute-start(s16[512,256]{1,0:T(8,128)(2,1)S(1)} %get-tuple-element.18.refs_0_), channel_id=1, source_target_pairs={{0,2},{2,0},{1,3},{3,1},{4,6},{6,4},{5,7},{7,5},{8,10},{10,8},{9,1... | collective-permute-start | bytes 786440 | tf_op jit(solution)/shard_map/ppermute | solution.py:268
  52.4 20.9 %collective-permute-start.7 = (s16[512,256]{1,0:T(8,128)(2,1)S(1)}, s16[512,256]{1,0:T(8,128)(2,1)S(1)}, u32[]{:S(2)}, u32[]{:S(2)}) collective-permute-start(s16[512,256]{1,0:T(8,128)(2,1)S(1)} %get-tuple-element.18.refs_0_), channel_id=1, source_target_pairs={{0,16},{8,24},{16,0},{24,8},{1,17},{9,25},{17,1},{25,9},{2,18},{10... | collective-permute-start | bytes 786440 | tf_op jit(solution)/shard_map/ppermute | solution.py:268
  56.6 18.8 %collective-permute-start.14 = (s16[512,256]{1,0:T(8,128)(2,1)S(1)}, s16[512,256]{1,0:T(8,128)(2,1)S(1)}, u32[]{:S(2)}, u32[]{:S(2)}) collective-permute-start(s16[512,256]{1,0:T(8,128)(2,1)S(1)} %collective-permute-done.13.refs_0_), channel_id=1, source_target_pairs={{0,2},{2,0},{1,3},{3,1},{4,6},{6,4},{5,7},{7,5},{8,10},{10,8},{9,1... | collective-permute-start | bytes 786440 | tf_op jit(solution)/shard_map/ppermute | solution.py:268
  57.6 17.9 %collective-permute-start.11 = (s16[512,256]{1,0:T(8,128)(2,1)S(1)}, s16[512,256]{1,0:T(8,128)(2,1)S(1)}, u32[]{:S(2)}, u32[]{:S(2)}) collective-permute-start(s16[512,256]{1,0:T(8,128)(2,1)S(1)} %collective-permute-done.10.refs_2_), channel_id=1, source_target_pairs={{0,2},{2,0},{1,3},{3,1},{4,6},{6,4},{5,7},{7,5},{8,10},{10,8},{9,1... | collective-permute-start | bytes 786440 | tf_op jit(solution)/shard_map/ppermute | solution.py:268
  62.0 14.7 %collective-permute-start.5 = (s16[512,256]{1,0:T(8,128)(2,1)S(1)}, s16[512,256]{1,0:T(8,128)(2,1)S(1)}, u32[]{:S(2)}, u32[]{:S(2)}) collective-permute-start(s16[512,256]{1,0:T(8,128)(2,1)S(1)} %collective-permute-done.2.refs_4_), channel_id=1, source_target_pairs={{0,2},{2,0},{1,3},{3,1},{4,6},{6,4},{5,7},{7,5},{8,10},{10,8},{9,1... | collective-permute-start | bytes 786440 | tf_op jit(solution)/shard_map/ppermute | solution.py:268
  62.7 15.5 %collective-permute-start.3 = (s16[512,256]{1,0:T(8,128)(2,1)S(1)}, s16[512,256]{1,0:T(8,128)(2,1)S(1)}, u32[]{:S(2)}, u32[]{:S(2)}) collective-permute-start(s16[512,256]{1,0:T(8,128)(2,1)S(1)} %collective-permute-done.2.refs_4_), channel_id=1, source_target_pairs={{0,4},{4,0},{1,5},{5,1},{2,6},{6,2},{3,7},{7,3},{8,12},{12,8},{9,1... | collective-permute-start | bytes 786440 | tf_op jit(solution)/shard_map/ppermute | solution.py:268
  73.3 11.3 %collective-permute-start.15 = (s16[512,256]{1,0:T(8,128)(2,1)S(1)}, s16[512,256]{1,0:T(8,128)(2,1)S(1)}, u32[]{:S(2)}, u32[]{:S(2)}) collective-permute-start(s16[512,256]{1,0:T(8,128)(2,1)S(1)} %collective-permute-done.13.refs_0_), channel_id=1, source_target_pairs={{0,4},{4,0},{1,5},{5,1},{2,6},{6,2},{3,7},{7,3},{8,12},{12,8},{9,1... | collective-permute-start | bytes 786440 | tf_op jit(solution)/shard_map/ppermute | solution.py:268
  75.5 12.8 %collective-permute-start.16 = (s16[512,256]{1,0:T(8,128)(2,1)S(1)}, s16[512,256]{1,0:T(8,128)(2,1)S(1)}, u32[]{:S(2)}, u32[]{:S(2)}) collective-permute-start(s16[512,256]{1,0:T(8,128)(2,1)S(1)} %collective-permute-done.14.refs_1_), channel_id=1, source_target_pairs={{0,4},{4,0},{1,5},{5,1},{2,6},{6,2},{3,7},{7,3},{8,12},{12,8},{9,1... | collective-permute-start | bytes 786440 | tf_op jit(solution)/shard_map/ppermute | solution.py:268
  75.5 22.3 %collective-permute-start.8 = (s16[512,256]{1,0:T(8,128)(2,1)S(1)}, s16[512,256]{1,0:T(8,128)(2,1)S(1)}, u32[]{:S(2)}, u32[]{:S(2)}) collective-permute-start(s16[512,256]{1,0:T(8,128)(2,1)S(1)} %collective-permute-done.7.refs_3_), channel_id=1, source_target_pairs={{0,2},{2,0},{1,3},{3,1},{4,6},{6,4},{5,7},{7,5},{8,10},{10,8},{9,1... | collective-permute-start | bytes 786440 | tf_op jit(solution)/shard_map/ppermute | solution.py:268
  76.7 21.1 %collective-permute-start.9 = (s16[512,256]{1,0:T(8,128)(2,1)S(1)}, s16[512,256]{1,0:T(8,128)(2,1)S(1)}, u32[]{:S(2)}, u32[]{:S(2)}) collective-permute-start(s16[512,256]{1,0:T(8,128)(2,1)S(1)} %collective-permute-done.7.refs_3_), channel_id=1, source_target_pairs={{0,4},{4,0},{1,5},{5,1},{2,6},{6,2},{3,7},{7,3},{8,12},{12,8},{9,1... | collective-permute-start | bytes 786440 | tf_op jit(solution)/shard_map/ppermute | solution.py:268
  78.2 19.6 %collective-permute-start.12 = (s16[512,256]{1,0:T(8,128)(2,1)S(1)}, s16[512,256]{1,0:T(8,128)(2,1)S(1)}, u32[]{:S(2)}, u32[]{:S(2)}) collective-permute-start(s16[512,256]{1,0:T(8,128)(2,1)S(1)} %collective-permute-done.11.refs_3_), channel_id=1, source_target_pairs={{0,16},{8,24},{16,0},{24,8},{1,17},{9,25},{17,1},{25,9},{2,18},{10... | collective-permute-start | bytes 786440 | tf_op jit(solution)/shard_map/ppermute | solution.py:268
  84.6 13.3 %collective-permute-start.4 = (s16[256,256]{1,0:T(8,128)(2,1)S(1)}, s16[256,256]{1,0:T(8,128)(2,1)S(1)}, u32[]{:S(2)}, u32[]{:S(2)}) collective-permute-start(s16[256,256]{1,0:T(8,128)(2,1)S(1)} %slice.8), channel_id=1, source_target_pairs={{0,2},{2,0},{1,3},{3,1},{4,6},{6,4},{5,7},{7,5},{8,10},{10,8},{9,1... | collective-permute-start | bytes 393224 | tf_op jit(solution)/shard_map/ppermute | solution.py:268
  88.2 9.6 %collective-permute-start.6 = (s16[256,256]{1,0:T(8,128)(2,1)S(1)}, s16[256,256]{1,0:T(8,128)(2,1)S(1)}, u32[]{:S(2)}, u32[]{:S(2)}) collective-permute-start(s16[256,256]{1,0:T(8,128)(2,1)S(1)} %slice.9), channel_id=1, source_target_pairs={{0,4},{4,0},{1,5},{5,1},{2,6},{6,2},{3,7},{7,3},{8,12},{12,8},{9,1... | collective-permute-start | bytes 393224 | tf_op jit(solution)/shard_map/ppermute | solution.py:268

commit v2 on v1

--- a/solution.py
+++ b/solution.py
@@ -15,7 +15,7 @@
 CODE_ROWS = 16
 LEVELS = 32767.0
 TINY = 1e-30
-GROUP = 8
+GROUP = 16
 SMALL_VMEM = 24 << 20
 F32, BF16, I32 = jnp.float32, jnp.bfloat16, jnp.int32
 HALF = LANES // 2
@@ -23,14 +23,20 @@
 OWNERS = ("z", "y", "x")
 AXES = ("g",) + OWNERS + ("mp",)
 
-SPREADS = ((0, 2), (2, 5), (5, 8))
+PAIRS = ((0, 0), (0, 1), (1, 0), (2, 0), (1, 1), (3, 0), (3, 1), (2, 1))
+SPREADS = ((0, 2), (2, 4), (4, 6), (6, 8))
 VMEM = pl.BlockSpec(memory_space=pltpu.VMEM)
 SMEM = pl.BlockSpec(memory_space=pltpu.SMEM)
 
 
-def pack_kernel(points_ref, assign_ref, keep_ref, out_ref):
+def pack_kernel(far_ref, assign_ref, keep_ref, out_ref, points_ref, sems):
     rows, width = points_ref.shape
     blocks = rows // LANES
+    copies = []
+    for b in range(blocks):
+        part = pl.ds(b * LANES, LANES)
+        copies.append(pltpu.make_async_copy(far_ref.at[part], points_ref.at[part], sems.at[b]))
+        copies[b].start()
     kept = keep_ref[...]
     assign = assign_ref[...]
     high = jnp.where(kept > 0, assign >> DIGIT, -1).astype(F32)
@@ -38,6 +44,7 @@
     weight = kept.astype(F32)
     peak = jnp.zeros((1, LANES), F32)
     for b in range(blocks):
+        copies[b].wait()
         for c in range(width // LANES):
             tile = points_ref[b * LANES : (b + 1) * LANES, c * LANES : (c + 1) * LANES].T
             out_ref[2 * c, b * COLS : (b + 1) * COLS, :] = tile[:COLS]
@@ -58,8 +65,9 @@
     return pl.pallas_call(
         pack_kernel,
         out_shape=jax.ShapeDtypeStruct(shape, BF16),
-        in_specs=[VMEM] * 3,
+        in_specs=[pl.BlockSpec(memory_space=pl.ANY), VMEM, VMEM],
         out_specs=VMEM,
+        scratch_shapes=[pltpu.VMEM((rows, width), BF16), pltpu.SemaphoreType.DMA((blocks,))],
         cost_estimate=pl.CostEstimate(
             flops=2 * rows * width, bytes_accessed=4 * rows * width, transcendentals=0
         ),
@@ -278,9 +286,7 @@
         [send(from_y[2][:half], "x"), send(from_x[2][half:], "y")],
         [send(near, "z", shifts[3])],
     ]
-    pairs = []
-    for n in range(nz):
-        pairs += [(held[n], [from_x[n]]), (from_y[n], diagonal[n])]
+    pairs = [(from_y[n], diagonal[n]) if m else (held[n], [from_x[n]]) for n, m in PAIRS]
     out = None
     for start, end in SPREADS:
         out = spread(start, pairs[start:end], where, peak, width, out)
@@ -302,16 +308,17 @@
     nz, ny, nx = (lax.axis_size(a) for a in OWNERS)
     assert nx == 2 and ny == 2 and nz * ny * nx * COLS == width
     block = z * ny + y
-    columns = [((z - s) % nz) * ny + (y ^ m) for s in z_shifts(nz) for m in range(ny)]
+    shifts = z_shifts(nz)
+    columns = [((z - shifts[n]) % nz) * ny + (y ^ m) for n, m in PAIRS]
     where = jnp.stack([lax.axis_index("mp") * shard_rows, x, *columns]).astype(I32)
 
-    parcels = pack(points, assign, keep_mask)
+    parcels, centroids = lax.optimization_barrier((pack(points, assign, keep_mask), centroids))
     recv = lax.all_to_all(parcels, OWNERS, 0, 0, tiled=True)
     others = lax.ppermute(centroids, "mp", SWAP)
 
     point_f = points.astype(F32)
     point_sq = jnp.sum(point_f * point_f, axis=1)
-    best = jnp.minimum(nearest(points, point_sq, centroids), nearest(points, point_sq, others))
+    best = jnp.minimum(nearest(points, point_sq, centroids), nearest(points, point_sq, others)) / width
     least = jnp.maximum(jnp.max(jnp.abs(centroids)).astype(F32), TINY)[None]
     prior = lax.dynamic_slice_in_dim(centroids, block * LANES, LANES, 1)
     recv, best, least, prior, where = lax.optimization_barrier((recv, best, least, prior, where))
@@ -327,7 +334,7 @@
         unit, peak = last_sums(partner, where, given, least, prior, high_size)
 
     out = gather(unit, peak, where, width)
-    return out, best / width
+    return out, best
 
 
 def split_dp(mesh, width):

time: 102 us -> 101 us (level)
  starting transfers between devices: 35.9 us -> 26.5 us
  waiting for transfers between devices: 23.6 us -> 30.1 us
  Pallas kernels: 21.4 us -> 22.5 us
    ppermute x16, starting transfers between devices: 27.5 us -> 18.1 us  [send(): lax.ppermute(piece, axis, [(i, (i + shift) % size) for i in range(size)])]
    ppermute x16, waiting for transfers between devices: 17.1 us -> 24.8 us  [send(): lax.ppermute(piece, axis, [(i, (i + shift) % size) for i in range(size)])]
    all_to_all x1, waiting for transfers between devices: 6.44 us -> 5.31 us  [shards(): recv = lax.all_to_all(parcels, OWNERS, 0, 0, tiled=True)]
    pallas_call x3 -> x4, Pallas kernels: 10.9 us -> 12 us  [spread(): pl.pallas_call(functools.partial(spread_kernel, tuple((len(others) for _,...]
  transfers between devices with their start and end apart: 19 -> 19, of which waited for: 7 -> 8; matrix products, arithmetic and copies ran while one was open for 19% -> 20% of each run, Pallas kernels for 13% -> 12%
where the time goes in v2:
time: 101 us
  waiting for transfers between devices  30.1 us (30%)
  starting transfers between devices  26.5 us (26%)
  Pallas kernels  22.5 us (22%)
  other arithmetic  11.1 us (11%)
  matrix products  7.44 us (7%)
  between operations  1.52 us (2%)
  local copies, waits for them, and re-layouts  1.36 us (1%)
    ppermute x16, waiting for transfers between devices, send(): lax.ppermute(piece, axis, [(i, (i + shift) % size) for i in range(size)])  24.8 us
    ppermute x16, starting transfers between devices, send(): lax.ppermute(piece, axis, [(i, (i + shift) % size) for i in range(size)])  18.1 us
    pallas_call x4, Pallas kernels, spread(): pl.pallas_call(functools.partial(spread_kernel, tuple((len(others) for _,...  12 us
    all_to_all x1, starting transfers between devices, shards(): recv = lax.all_to_all(parcels, OWNERS, 0, 0, tiled=True)  7.88 us
    dot_general x2, matrix products, nearest(): lax.dot_general(points, part, (((1,), (1,)), ((), ())), preferred_element...  7.44 us
    reduce_sum x2, other arithmetic, nearest(): part_sq = jnp.sum(part_f * part_f, axis=1)  6.35 us
    all_to_all x1, waiting for transfers between devices, shards(): recv = lax.all_to_all(parcels, OWNERS, 0, 0, tiled=True)  5.31 us
    pallas_call x1, Pallas kernels, last_sums(): pl.pallas_call(last_kernel, out_shape=(unit_shape(high_size), jax.ShapeDt...  4.2 us
  transfers between devices with their start and end apart: 19, of which 8 were waited for; matrix products, arithmetic and copies ran while one was open for 20% of the time, Pallas kernels for 12%

profile of v2, /device:TPU:0, one launch (start us, length us, event | category | flops | bytes accessed | tf_op | source)
XLA Modules:
  0.0 100.6 jit_solution(17062832942687091073)
XLA Ops:
  0.6 3.2 %pack.1 = bf16[16,272,128]{2,1,0:T(8,128)(2,1)} custom-call(bf16[512,1024]{1,0:T(8,128)(2,1)} %far_ref.1, s32[4,128]{1,0:T(4,128)} %bitcast.17, s32[4,128]{1,0:T(4,128)} %bitcast.18), custom_call_target="tpu_custom_call" | custom-call | flops 1048576 | bytes 2097152 | tf_op jit(solution)/shard_map/pack/pallas_call | solution.py:65
  3.9 0.6 collective-permute-start
  4.4 7.9 %all-to-all-start = ((bf16[16,272,128]{2,1,0:T(8,128)(2,1)}), bf16[16,272,128]{2,1,0:T(8,128)(2,1)S(1)}, u32[]{:S(2)}, u32[]{:S(2)}) async-start(bf16[16,272,128]{2,1,0:T(8,128)(2,1)} %pack.1), calls=%async_computation | async-start | bytes 2228224 | tf_op jit(solution)/shard_map/all_to_all | solution.py:316
  12.4 0.0 copy-start.1
  12.4 3.9 %abs_reduce_fusion = bf16[]{:T(256)} fusion(bf16[2048,1024]{1,0:T(8,128)(2,1)} %param.5), kind=kLoop, calls=%fused_computation.2 | loop fusion | flops 4194303 | bytes 4194306 | tf_op jit(solution)/shard_map/reduce_max | solution.py:322
  17.0 0.1 stack.43.where_ref
  17.1 1.2 %constant_dynamic-slice_fusion.prior_ref = bf16[2048,128]{1,0:T(8,128)(2,1)S(1)} fusion(bf16[2048,1024]{1,0:T(8,128)(2,1)} %param.5, s32[]{:T(128)S(6)} %select_n.30), kind=kLoop, calls=%fused_computation.7 | loop fusion | bytes 1048580 | tf_op jit(solution)/shard_map/dynamic_slice | solution.py:323
  18.3 3.3 %multiply_reduce_fusion.1 = f32[2048]{0:T(1024)S(1)} fusion(bf16[2048,1024]{1,0:T(8,128)(2,1)} %param.5), kind=kLoop, calls=%fused_computation.1 | loop fusion | flops 6289408 | bytes 4202496 | tf_op jit(solution)/shard_map/reduce_sum | solution.py:299
  21.6 0.3 multiply_reduce_fusion.2
  21.9 2.6 %add_reduce_fusion.1 = f32[512]{0:T(512)S(1)} fusion(bf16[2048,1024]{1,0:T(8,128)(2,1)S(1)} %copy-done, bf16[512,1024]{1,0:T(8,128)(2,1)S(1)} %copy-done.1, f32[2048]{0:T(1024)S(1)} %multiply_reduce_fusion.1, f32[512]{0:T(512)S(1)} %multiply_reduce_fusion.2), kind=kOutput, calls=%fused_computation.4 | convolution fusion | flops 2151677440 | bytes 5255168 | tf_op jit(solution)/shard_map/dot_general | solution.py:297
  24.5 0.0 collective-permute-done
  24.5 3.1 %multiply_reduce_fusion = f32[2048]{0:T(1024)S(1)} fusion(bf16[2048,1024]{1,0:T(8,128)(2,1)} %collective-permute-done), kind=kLoop, calls=%fused_computation | loop fusion | flops 6289408 | bytes 4202496 | tf_op jit(solution)/shard_map/reduce_sum | solution.py:299
  27.6 4.8 %add_reduce_fusion = f32[512]{0:T(512)S(1)} fusion(f32[2048]{0:T(1024)S(1)} %multiply_reduce_fusion, f32[512]{0:T(512)S(1)} %multiply_reduce_fusion.2, bf16[2048,1024]{1,0:T(8,128)(2,1)} %collective-permute-done, bf16[512,1024]{1,0:T(8,128)(2,1)S(1)} %copy-done.1), kind=kOutput, calls=%fused_computation.3 | convolution fusion | flops 2151677440 | bytes 5255168 | tf_op jit(solution)/shard_map/dot_general | solution.py:297
  32.5 0.6 minimum_multiply_fusion
  33.0 5.3 %all-to-all-done.recv_ref = bf16[16,272,128]{2,1,0:T(8,128)(2,1)S(1)} async-done(((bf16[16,272,128]{2,1,0:T(8,128)(2,1)}), bf16[16,272,128]{2,1,0:T(8,128)(2,1)S(1)}, u32[]{:S(2)}, u32[]{:S(2)}) %all-to-all-start) | async-done | bytes 1114144 | tf_op jit(solution)/shard_map/all_to_all | solution.py:316
  38.3 0.0 collective-permute-start.1
  38.4 3.0 %sums_first.1 = (f32[272,512]{1,0:T(8,128)S(1)}, f32[8,128]{1,0:T(8,128)S(1)}) custom-call(s32[10]{0:T(128)S(1)} %stack.43.where_ref, bf16[16,272,128]{2,1,0:T(8,128)(2,1)S(1)} %all-to-all-done.recv_ref), custom_call_target="tpu_custom_call" | custom-call | flops 2281701376 | bytes 1114112 | tf_op jit(solution)/shard_map/sums_first/pallas_call | solution.py:171
  41.4 4.2 %sums_last.1 = (s16[512,256]{1,0:T(8,128)(2,1)S(1)}, f32[1]{0:T(128)}) custom-call(s32[10]{0:T(128)S(1)} %stack.43.where_ref, f32[1]{0:T(128)} %bitcast.2.least_ref, bf16[16,272,128]{2,1,0:T(8,128)(2,1)S(1)} %collective-permute-done.1.recv_ref, f32[272,512]{1,0:T(8,128)S(1)} %get-tuple-element.18.given_ref, f32[8,128]{1,0:T(8,128)S(1)} %get-tuple-element.19.given_peak_ref, ...), custom_call_target="tpu_custom_call" | custom-call | flops 2281701376 | bytes 1114112 | tf_op jit(solution)/shard_map/sums_last/pallas_call | solution.py:187
  45.6 2.1 %collective-permute-start.4 = (s16[512,256]{1,0:T(8,128)(2,1)S(1)}, s16[512,256]{1,0:T(8,128)(2,1)S(1)}, u32[]{:S(2)}, u32[]{:S(2)}) collective-permute-start(s16[512,256]{1,0:T(8,128)(2,1)S(1)} %get-tuple-element.22.refs_0_), channel_id=1, source_target_pairs={{0,4},{4,0},{1,5},{5,1},{2,6},{6,2},{3,7},{7,3},{8,12},{12,8},{9,1... | collective-permute-start | bytes 786440 | tf_op jit(solution)/shard_map/ppermute | solution.py:276
  47.8 2.8 %collective-permute-start.12 = (s16[512,256]{1,0:T(8,128)(2,1)S(1)}, s16[512,256]{1,0:T(8,128)(2,1)S(1)}, u32[]{:S(2)}, u32[]{:S(2)}) collective-permute-start(s16[512,256]{1,0:T(8,128)(2,1)S(1)} %get-tuple-element.22.refs_0_), channel_id=1, source_target_pairs={{0,8},{8,16},{16,24},{24,0},{1,9},{9,17},{17,25},{25,1},{2,10},{10... | collective-permute-start | bytes 786440 | tf_op jit(solution)/shard_map/ppermute | solution.py:276
  50.5 1.2 %collective-permute-start.7 = (s16[512,256]{1,0:T(8,128)(2,1)S(1)}, s16[512,256]{1,0:T(8,128)(2,1)S(1)}, u32[]{:S(2)}, u32[]{:S(2)}) collective-permute-start(s16[512,256]{1,0:T(8,128)(2,1)S(1)} %get-tuple-element.22.refs_0_), channel_id=1, source_target_pairs={{0,24},{8,0},{16,8},{24,16},{1,25},{9,1},{17,9},{25,17},{2,26},{10... | collective-permute-start | bytes 786440 | tf_op jit(solution)/shard_map/ppermute | solution.py:276
  51.7 0.7 collective-permute-start.17
  52.4 0.5 collective-permute-start.2
  53.0 1.8 %collective-permute-done.4.refs_2_ = s16[512,256]{1,0:T(8,128)(2,1)S(1)} collective-permute-done((s16[512,256]{1,0:T(8,128)(2,1)S(1)}, s16[512,256]{1,0:T(8,128)(2,1)S(1)}, u32[]{:S(2)}, u32[]{:S(2)}) %collective-permute-start.4) | collective-permute-done | bytes 262176 | tf_op jit(solution)/shard_map/ppermute | solution.py:276
  54.7 0.9 collective-permute-start.5
  55.6 3.3 %collective-permute-done.12.refs_0_ = s16[512,256]{1,0:T(8,128)(2,1)S(1)} collective-permute-done((s16[512,256]{1,0:T(8,128)(2,1)S(1)}, s16[512,256]{1,0:T(8,128)(2,1)S(1)}, u32[]{:S(2)}, u32[]{:S(2)}) %collective-permute-start.12) | collective-permute-done | bytes 262176 | tf_op jit(solution)/shard_map/ppermute | solution.py:276
  58.9 0.7 collective-permute-start.14
  59.6 4.4 %collective-permute-done.7.refs_2_ = s16[512,256]{1,0:T(8,128)(2,1)S(1)} collective-permute-done((s16[512,256]{1,0:T(8,128)(2,1)S(1)}, s16[512,256]{1,0:T(8,128)(2,1)S(1)}, u32[]{:S(2)}, u32[]{:S(2)}) %collective-permute-start.7) | collective-permute-done | bytes 262176 | tf_op jit(solution)/shard_map/ppermute | solution.py:276
  64.0 0.7 collective-permute-start.10
  64.7 0.0 collective-permute-done.17.refs_1_
  64.7 0.3 collective-permute-start.8
  65.0 10.2 %collective-permute-done.2.refs_2_ = s16[512,256]{1,0:T(8,128)(2,1)S(1)} collective-permute-done((s16[512,256]{1,0:T(8,128)(2,1)S(1)}, s16[512,256]{1,0:T(8,128)(2,1)S(1)}, u32[]{:S(2)}, u32[]{:S(2)}) %collective-permute-start.2) | collective-permute-done | bytes 262176 | tf_op jit(solution)/shard_map/ppermute | solution.py:276
  75.2 0.3 collective-permute-start.13
  75.6 0.7 collective-permute-start.16
  76.3 0.0 collective-permute-done.14.refs_1_
  76.3 1.7 %collective-permute-start.15 = (s16[512,256]{1,0:T(8,128)(2,1)S(1)}, s16[512,256]{1,0:T(8,128)(2,1)S(1)}, u32[]{:S(2)}, u32[]{:S(2)}) collective-permute-start(s16[512,256]{1,0:T(8,128)(2,1)S(1)} %collective-permute-done.14.refs_1_), channel_id=1, source_target_pairs={{0,4},{4,0},{1,5},{5,1},{2,6},{6,2},{3,7},{7,3},{8,12},{12,8},{9,1... | collective-permute-start | bytes 786440 | tf_op jit(solution)/shard_map/ppermute | solution.py:276
  78.0 0.3 collective-permute-start.3
  78.3 4.0 %collective-permute-start.6 = (s16[512,256]{1,0:T(8,128)(2,1)S(1)}, s16[512,256]{1,0:T(8,128)(2,1)S(1)}, u32[]{:S(2)}, u32[]{:S(2)}) collective-permute-start(s16[512,256]{1,0:T(8,128)(2,1)S(1)} %collective-permute-done.5.refs_3_), channel_id=1, source_target_pairs={{0,16},{8,24},{16,0},{24,8},{1,17},{9,25},{17,1},{25,9},{2,18},{10... | collective-permute-start | bytes 786440 | tf_op jit(solution)/shard_map/ppermute | solution.py:276
  82.3 2.1 %collective-permute-done.13.refs_0_ = s16[512,256]{1,0:T(8,128)(2,1)S(1)} collective-permute-done((s16[512,256]{1,0:T(8,128)(2,1)S(1)}, s16[512,256]{1,0:T(8,128)(2,1)S(1)}, u32[]{:S(2)}, u32[]{:S(2)}) %collective-permute-start.13) | collective-permute-done | bytes 262176 | tf_op jit(solution)/shard_map/ppermute | solution.py:276
  84.4 0.3 collective-permute-start.11
  84.8 0.7 collective-permute-start.9
  85.5 3.0 %spread.4.refs_4_ = f32[2048,1024]{1,0:T(8,128)} custom-call(s32[10]{0:T(128)S(1)} %stack.43.where_ref, f32[1]{0:T(128)} %get-tuple-element.21.peak_ref, s16[512,256]{1,0:T(8,128)(2,1)S(1)} %get-tuple-element.22.refs_0_, s16[512,256]{1,0:T(8,128)(2,1)S(1)} %collective-permute-done.17.refs_1_, s16[512,256]{1,0:T(8,128)(2,1)S(1)} %collective-permute-done.4.refs_2_, ...), custom_call_target="tpu_custom_call" | custom-call | flops 4194304 | bytes 3145728 | tf_op jit(solution)/shard_map/spread/pallas_call | solution.py:245
  88.5 3.0 %spread.5.refs_4_ = f32[2048,1024]{1,0:T(8,128)} custom-call(s32[10]{0:T(128)S(1)} %stack.43.where_ref, f32[1]{0:T(128)} %get-tuple-element.21.peak_ref, s16[512,256]{1,0:T(8,128)(2,1)S(1)} %collective-permute-done.12.refs_0_, s16[512,256]{1,0:T(8,128)(2,1)S(1)} %collective-permute-done.14.refs_1_, ...), custom_call_target="tpu_custom_call", output_to_operand_aliasing={{}: (6, {})} | custom-call | flops 4194304 | bytes 3145728 | tf_op jit(solution)/shard_map/spread/pallas_call | solution.py:245
  91.5 0.0 collective-permute-done.15.refs_1_
  91.5 3.0 %spread.6.refs_5_ = f32[2048,1024]{1,0:T(8,128)} custom-call(s32[10]{0:T(128)S(1)} %stack.43.where_ref, f32[1]{0:T(128)} %get-tuple-element.21.peak_ref, s16[512,256]{1,0:T(8,128)(2,1)S(1)} %collective-permute-done.13.refs_0_, s16[512,256]{1,0:T(8,128)(2,1)S(1)} %collective-permute-done.15.refs_1_, ...), custom_call_target="tpu_custom_call", output_to_operand_aliasing={{}: (6, {})} | custom-call | flops 4194304 | bytes 3145728 | tf_op jit(solution)/shard_map/spread/pallas_call | solution.py:245
  94.5 1.2 %collective-permute-done.3.refs_0_ = s16[512,256]{1,0:T(8,128)(2,1)S(1)} collective-permute-done((s16[512,256]{1,0:T(8,128)(2,1)S(1)}, s16[512,256]{1,0:T(8,128)(2,1)S(1)}, u32[]{:S(2)}, u32[]{:S(2)}) %collective-permute-start.3) | collective-permute-done | bytes 262176 | tf_op jit(solution)/shard_map/ppermute | solution.py:276
  95.7 1.9 %collective-permute-done.11.refs_4_ = s16[256,256]{1,0:T(8,128)(2,1)S(1)} collective-permute-done((s16[256,256]{1,0:T(8,128)(2,1)S(1)}, s16[256,256]{1,0:T(8,128)(2,1)S(1)}, u32[]{:S(2)}, u32[]{:S(2)}) %collective-permute-start.11) | collective-permute-done | bytes 131104 | tf_op jit(solution)/shard_map/ppermute | solution.py:276
  97.5 3.0 %spread.7 = f32[2048,1024]{1,0:T(8,128)} custom-call(s32[10]{0:T(128)S(1)} %stack.43.where_ref, f32[1]{0:T(128)} %get-tuple-element.21.peak_ref, s16[512,256]{1,0:T(8,128)(2,1)S(1)} %collective-permute-done.3.refs_0_, s16[512,256]{1,0:T(8,128)(2,1)S(1)} %collective-permute-done.6.refs_1_, ...), custom_call_target="tpu_custom_call", output_to_operand_aliasing={{}: (7, {})} | custom-call | flops 4194304 | bytes 3145728 | tf_op jit(solution)/shard_map/spread/pallas_call | solution.py:245
  (12 shorter events, 0.0 us)
Async XLA Ops:
  3.9 20.7 %collective-permute-start = (bf16[2048,1024]{1,0:T(8,128)(2,1)}, bf16[2048,1024]{1,0:T(8,128)(2,1)}, u32[]{:S(2)}, u32[]{:S(2)}) collective-permute-start(bf16[2048,1024]{1,0:T(8,128)(2,1)} %param.5), channel_id=1, source_target_pairs={{0,1},{1,0},{2,3},{3,2},{4,5},{5,4},{6,7},{7,6},{8,9},{9,8},{10,11... | collective-permute-start | bytes 12582920 | tf_op jit(solution)/shard_map/ppermute | solution.py:317
  4.4 33.9 %all-to-all-start = ((bf16[16,272,128]{2,1,0:T(8,128)(2,1)}), bf16[16,272,128]{2,1,0:T(8,128)(2,1)S(1)}, u32[]{:S(2)}, u32[]{:S(2)}) async-start(bf16[16,272,128]{2,1,0:T(8,128)(2,1)} %pack.1), calls=%async_computation | async-start | bytes 2228224 | tf_op jit(solution)/shard_map/all_to_all | solution.py:316
  12.4 9.2 %copy-start.1 = (bf16[512,1024]{1,0:T(8,128)(2,1)S(1)}, bf16[512,1024]{1,0:T(8,128)(2,1)}, u32[]{:S(2)}) copy-start(bf16[512,1024]{1,0:T(8,128)(2,1)} %far_ref.1) | copy-start | bytes 3145732
  17.1 4.8 %copy-start = (bf16[2048,1024]{1,0:T(8,128)(2,1)S(1)}, bf16[2048,1024]{1,0:T(8,128)(2,1)}, u32[]{:S(2)}) copy-start(bf16[2048,1024]{1,0:T(8,128)(2,1)} %param.5) | copy-start | bytes 12582916
  38.3 3.1 %collective-permute-start.1 = (bf16[16,272,128]{2,1,0:T(8,128)(2,1)S(1)}, bf16[16,272,128]{2,1,0:T(8,128)(2,1)S(1)}, u32[]{:S(2)}, u32[]{:S(2)}) collective-permute-start(bf16[16,272,128]{2,1,0:T(8,128)(2,1)S(1)} %all-to-all-done.recv_ref), channel_id=1, source_target_pairs={{0,1},{1,0},{2,3},{3,2},{4,5},{5,4},{6,7},{7,6},{8,9},{9,8},{10,11... | collective-permute-start | bytes 3342344 | tf_op jit(solution)/shard_map/ppermute | solution.py:326
  45.6 9.1 %collective-permute-start.4 = (s16[512,256]{1,0:T(8,128)(2,1)S(1)}, s16[512,256]{1,0:T(8,128)(2,1)S(1)}, u32[]{:S(2)}, u32[]{:S(2)}) collective-permute-start(s16[512,256]{1,0:T(8,128)(2,1)S(1)} %get-tuple-element.22.refs_0_), channel_id=1, source_target_pairs={{0,4},{4,0},{1,5},{5,1},{2,6},{6,2},{3,7},{7,3},{8,12},{12,8},{9,1... | collective-permute-start | bytes 786440 | tf_op jit(solution)/shard_map/ppermute | solution.py:276
  47.8 11.1 %collective-permute-start.12 = (s16[512,256]{1,0:T(8,128)(2,1)S(1)}, s16[512,256]{1,0:T(8,128)(2,1)S(1)}, u32[]{:S(2)}, u32[]{:S(2)}) collective-permute-start(s16[512,256]{1,0:T(8,128)(2,1)S(1)} %get-tuple-element.22.refs_0_), channel_id=1, source_target_pairs={{0,8},{8,16},{16,24},{24,0},{1,9},{9,17},{17,25},{25,1},{2,10},{10... | collective-permute-start | bytes 786440 | tf_op jit(solution)/shard_map/ppermute | solution.py:276
  50.5 13.5 %collective-permute-start.7 = (s16[512,256]{1,0:T(8,128)(2,1)S(1)}, s16[512,256]{1,0:T(8,128)(2,1)S(1)}, u32[]{:S(2)}, u32[]{:S(2)}) collective-permute-start(s16[512,256]{1,0:T(8,128)(2,1)S(1)} %get-tuple-element.22.refs_0_), channel_id=1, source_target_pairs={{0,24},{8,0},{16,8},{24,16},{1,25},{9,1},{17,9},{25,17},{2,26},{10... | collective-permute-start | bytes 786440 | tf_op jit(solution)/shard_map/ppermute | solution.py:276
  51.7 13.0 %collective-permute-start.17 = (s16[512,256]{1,0:T(8,128)(2,1)S(1)}, s16[512,256]{1,0:T(8,128)(2,1)S(1)}, u32[]{:S(2)}, u32[]{:S(2)}) collective-permute-start(s16[512,256]{1,0:T(8,128)(2,1)S(1)} %get-tuple-element.22.refs_0_), channel_id=1, source_target_pairs={{0,2},{2,0},{1,3},{3,1},{4,6},{6,4},{5,7},{7,5},{8,10},{10,8},{9,1... | collective-permute-start | bytes 786440 | tf_op jit(solution)/shard_map/ppermute | solution.py:276
  52.4 22.8 %collective-permute-start.2 = (s16[512,256]{1,0:T(8,128)(2,1)S(1)}, s16[512,256]{1,0:T(8,128)(2,1)S(1)}, u32[]{:S(2)}, u32[]{:S(2)}) collective-permute-start(s16[512,256]{1,0:T(8,128)(2,1)S(1)} %get-tuple-element.22.refs_0_), channel_id=1, source_target_pairs={{0,16},{8,24},{16,0},{24,8},{1,17},{9,25},{17,1},{25,9},{2,18},{10... | collective-permute-start | bytes 786440 | tf_op jit(solution)/shard_map/ppermute | solution.py:276
  54.7 20.9 %collective-permute-start.5 = (s16[512,256]{1,0:T(8,128)(2,1)S(1)}, s16[512,256]{1,0:T(8,128)(2,1)S(1)}, u32[]{:S(2)}, u32[]{:S(2)}) collective-permute-start(s16[512,256]{1,0:T(8,128)(2,1)S(1)} %collective-permute-done.4.refs_2_), channel_id=1, source_target_pairs={{0,2},{2,0},{1,3},{3,1},{4,6},{6,4},{5,7},{7,5},{8,10},{10,8},{9,1... | collective-permute-start | bytes 786440 | tf_op jit(solution)/shard_map/ppermute | solution.py:276
  58.9 17.4 %collective-permute-start.14 = (s16[512,256]{1,0:T(8,128)(2,1)S(1)}, s16[512,256]{1,0:T(8,128)(2,1)S(1)}, u32[]{:S(2)}, u32[]{:S(2)}) collective-permute-start(s16[512,256]{1,0:T(8,128)(2,1)S(1)} %collective-permute-done.12.refs_0_), channel_id=1, source_target_pairs={{0,2},{2,0},{1,3},{3,1},{4,6},{6,4},{5,7},{7,5},{8,10},{10,8},{9,1... | collective-permute-start | bytes 786440 | tf_op jit(solution)/shard_map/ppermute | solution.py:276
  64.0 14.0 %collective-permute-start.10 = (s16[512,256]{1,0:T(8,128)(2,1)S(1)}, s16[512,256]{1,0:T(8,128)(2,1)S(1)}, u32[]{:S(2)}, u32[]{:S(2)}) collective-permute-start(s16[512,256]{1,0:T(8,128)(2,1)S(1)} %collective-permute-done.7.refs_2_), channel_id=1, source_target_pairs={{0,2},{2,0},{1,3},{3,1},{4,6},{6,4},{5,7},{7,5},{8,10},{10,8},{9,1... | collective-permute-start | bytes 786440 | tf_op jit(solution)/shard_map/ppermute | solution.py:276
  64.7 13.6 %collective-permute-start.8 = (s16[512,256]{1,0:T(8,128)(2,1)S(1)}, s16[512,256]{1,0:T(8,128)(2,1)S(1)}, u32[]{:S(2)}, u32[]{:S(2)}) collective-permute-start(s16[512,256]{1,0:T(8,128)(2,1)S(1)} %collective-permute-done.7.refs_2_), channel_id=1, source_target_pairs={{0,4},{4,0},{1,5},{5,1},{2,6},{6,2},{3,7},{7,3},{8,12},{12,8},{9,1... | collective-permute-start | bytes 786440 | tf_op jit(solution)/shard_map/ppermute | solution.py:276
  75.2 9.2 %collective-permute-start.13 = (s16[512,256]{1,0:T(8,128)(2,1)S(1)}, s16[512,256]{1,0:T(8,128)(2,1)S(1)}, u32[]{:S(2)}, u32[]{:S(2)}) collective-permute-start(s16[512,256]{1,0:T(8,128)(2,1)S(1)} %collective-permute-done.12.refs_0_), channel_id=1, source_target_pairs={{0,4},{4,0},{1,5},{5,1},{2,6},{6,2},{3,7},{7,3},{8,12},{12,8},{9,1... | collective-permute-start | bytes 786440 | tf_op jit(solution)/shard_map/ppermute | solution.py:276
  75.6 9.2 %collective-permute-start.16 = (s16[512,256]{1,0:T(8,128)(2,1)S(1)}, s16[512,256]{1,0:T(8,128)(2,1)S(1)}, u32[]{:S(2)}, u32[]{:S(2)}) collective-permute-start(s16[512,256]{1,0:T(8,128)(2,1)S(1)} %collective-permute-done.2.refs_2_), channel_id=1, source_target_pairs={{0,2},{2,0},{1,3},{3,1},{4,6},{6,4},{5,7},{7,5},{8,10},{10,8},{9,1... | collective-permute-start | bytes 786440 | tf_op jit(solution)/shard_map/ppermute | solution.py:276
  76.3 15.2 %collective-permute-start.15 = (s16[512,256]{1,0:T(8,128)(2,1)S(1)}, s16[512,256]{1,0:T(8,128)(2,1)S(1)}, u32[]{:S(2)}, u32[]{:S(2)}) collective-permute-start(s16[512,256]{1,0:T(8,128)(2,1)S(1)} %collective-permute-done.14.refs_1_), channel_id=1, source_target_pairs={{0,4},{4,0},{1,5},{5,1},{2,6},{6,2},{3,7},{7,3},{8,12},{12,8},{9,1... | collective-permute-start | bytes 786440 | tf_op jit(solution)/shard_map/ppermute | solution.py:276
  78.0 17.7 %collective-permute-start.3 = (s16[512,256]{1,0:T(8,128)(2,1)S(1)}, s16[512,256]{1,0:T(8,128)(2,1)S(1)}, u32[]{:S(2)}, u32[]{:S(2)}) collective-permute-start(s16[512,256]{1,0:T(8,128)(2,1)S(1)} %collective-permute-done.2.refs_2_), channel_id=1, source_target_pairs={{0,4},{4,0},{1,5},{5,1},{2,6},{6,2},{3,7},{7,3},{8,12},{12,8},{9,1... | collective-permute-start | bytes 786440 | tf_op jit(solution)/shard_map/ppermute | solution.py:276
  78.3 19.2 %collective-permute-start.6 = (s16[512,256]{1,0:T(8,128)(2,1)S(1)}, s16[512,256]{1,0:T(8,128)(2,1)S(1)}, u32[]{:S(2)}, u32[]{:S(2)}) collective-permute-start(s16[512,256]{1,0:T(8,128)(2,1)S(1)} %collective-permute-done.5.refs_3_), channel_id=1, source_target_pairs={{0,16},{8,24},{16,0},{24,8},{1,17},{9,25},{17,1},{25,9},{2,18},{10... | collective-permute-start | bytes 786440 | tf_op jit(solution)/shard_map/ppermute | solution.py:276
  84.4 13.1 %collective-permute-start.11 = (s16[256,256]{1,0:T(8,128)(2,1)S(1)}, s16[256,256]{1,0:T(8,128)(2,1)S(1)}, u32[]{:S(2)}, u32[]{:S(2)}) collective-permute-start(s16[256,256]{1,0:T(8,128)(2,1)S(1)} %slice.9), channel_id=1, source_target_pairs={{0,4},{4,0},{1,5},{5,1},{2,6},{6,2},{3,7},{7,3},{8,12},{12,8},{9,1... | collective-permute-start | bytes 393224 | tf_op jit(solution)/shard_map/ppermute | solution.py:276
  84.8 12.8 %collective-permute-start.9 = (s16[256,256]{1,0:T(8,128)(2,1)S(1)}, s16[256,256]{1,0:T(8,128)(2,1)S(1)}, u32[]{:S(2)}, u32[]{:S(2)}) collective-permute-start(s16[256,256]{1,0:T(8,128)(2,1)S(1)} %slice.8), channel_id=1, source_target_pairs={{0,2},{2,0},{1,3},{3,1},{4,6},{6,4},{5,7},{7,5},{8,10},{10,8},{9,1... | collective-permute-start | bytes 393224 | tf_op jit(solution)/shard_map/ppermute | solution.py:276

commit v3 on v2

--- a/solution.py
+++ b/solution.py
@@ -29,14 +29,9 @@
 SMEM = pl.BlockSpec(memory_space=pltpu.SMEM)
 
 
-def pack_kernel(far_ref, assign_ref, keep_ref, out_ref, points_ref, sems):
+def pack_kernel(points_ref, assign_ref, keep_ref, out_ref):
     rows, width = points_ref.shape
     blocks = rows // LANES
-    copies = []
-    for b in range(blocks):
-        part = pl.ds(b * LANES, LANES)
-        copies.append(pltpu.make_async_copy(far_ref.at[part], points_ref.at[part], sems.at[b]))
-        copies[b].start()
     kept = keep_ref[...]
     assign = assign_ref[...]
     high = jnp.where(kept > 0, assign >> DIGIT, -1).astype(F32)
@@ -44,7 +39,6 @@
     weight = kept.astype(F32)
     peak = jnp.zeros((1, LANES), F32)
     for b in range(blocks):
-        copies[b].wait()
         for c in range(width // LANES):
             tile = points_ref[b * LANES : (b + 1) * LANES, c * LANES : (c + 1) * LANES].T
             out_ref[2 * c, b * COLS : (b + 1) * COLS, :] = tile[:COLS]
@@ -65,9 +59,8 @@
     return pl.pallas_call(
         pack_kernel,
         out_shape=jax.ShapeDtypeStruct(shape, BF16),
-        in_specs=[pl.BlockSpec(memory_space=pl.ANY), VMEM, VMEM],
+        in_specs=[VMEM] * 3,
         out_specs=VMEM,
-        scratch_shapes=[pltpu.VMEM((rows, width), BF16), pltpu.SemaphoreType.DMA((blocks,))],
         cost_estimate=pl.CostEstimate(
             flops=2 * rows * width, bytes_accessed=4 * rows * width, transcendentals=0
         ),

time: 101 us -> 100 us (0.990)
  no operation moved by 1% of the time
where the time goes in v3:
time: 100 us; the launch traced here: 99.9 us
  waiting for transfers between devices  30.2 us (30%)
  starting transfers between devices  26.4 us (26%)
  Pallas kernels  21.9 us (22%)
  other arithmetic  11.1 us (11%)
  matrix products  7.45 us (7%)
  between operations  1.51 us (2%)
  local copies, waits for them, and re-layouts  1.36 us (1%)
    ppermute x16, waiting for transfers between devices, send(): lax.ppermute(piece, axis, [(i, (i + shift) % size) for i in range(size)])  24.9 us
    ppermute x16, starting transfers between devices, send(): lax.ppermute(piece, axis, [(i, (i + shift) % size) for i in range(size)])  18 us
    pallas_call x4, Pallas kernels, spread(): pl.pallas_call(functools.partial(spread_kernel, tuple((len(others) for _,...  12 us
    all_to_all x1, starting transfers between devices, shards(): recv = lax.all_to_all(parcels, OWNERS, 0, 0, tiled=True)  7.85 us
    dot_general x2, matrix products, nearest(): lax.dot_general(points, part, (((1,), (1,)), ((), ())), preferred_element...  7.45 us
    reduce_sum x2, other arithmetic, nearest(): part_sq = jnp.sum(part_f * part_f, axis=1)  6.35 us
    all_to_all x1, waiting for transfers between devices, shards(): recv = lax.all_to_all(parcels, OWNERS, 0, 0, tiled=True)  5.33 us
    pallas_call x1, Pallas kernels, last_sums(): pl.pallas_call(last_kernel, out_shape=(unit_shape(high_size), jax.ShapeDt...  4.21 us
  transfers between devices with their start and end apart: 19, of which 8 were waited for; matrix products, arithmetic and copies ran while one was open for 20% of the time, Pallas kernels for 12%

profile of v3, /device:TPU:0, one launch (start us, length us, event | category | flops | bytes accessed | tf_op | source)
XLA Modules:
  0.0 99.9 jit_solution(16998972552282769188)
XLA Ops:
  0.6 2.6 %pack.1 = bf16[16,272,128]{2,1,0:T(8,128)(2,1)} custom-call(bf16[512,1024]{1,0:T(8,128)(2,1)} %points_ref.1, s32[4,128]{1,0:T(4,128)} %bitcast.17, s32[4,128]{1,0:T(4,128)} %bitcast.18), custom_call_target="tpu_custom_call" | custom-call | flops 1048576 | bytes 2097152 | tf_op jit(solution)/shard_map/pack/pallas_call | solution.py:59
  3.2 0.5 collective-permute-start
  3.7 7.9 %all-to-all-start = ((bf16[16,272,128]{2,1,0:T(8,128)(2,1)}), bf16[16,272,128]{2,1,0:T(8,128)(2,1)S(1)}, u32[]{:S(2)}, u32[]{:S(2)}) async-start(bf16[16,272,128]{2,1,0:T(8,128)(2,1)} %pack.1), calls=%async_computation | async-start | bytes 2228224 | tf_op jit(solution)/shard_map/all_to_all | solution.py:309
  11.6 0.0 copy-start.1
  11.6 3.9 %abs_reduce_fusion = bf16[]{:T(256)} fusion(bf16[2048,1024]{1,0:T(8,128)(2,1)} %param.5), kind=kLoop, calls=%fused_computation.2 | loop fusion | flops 4194303 | bytes 4194306 | tf_op jit(solution)/shard_map/reduce_max | solution.py:315
  16.3 0.1 stack.43.where_ref
  16.4 1.2 %constant_dynamic-slice_fusion.prior_ref = bf16[2048,128]{1,0:T(8,128)(2,1)S(1)} fusion(bf16[2048,1024]{1,0:T(8,128)(2,1)} %param.5, s32[]{:T(128)S(6)} %select_n.30), kind=kLoop, calls=%fused_computation.7 | loop fusion | bytes 1048580 | tf_op jit(solution)/shard_map/dynamic_slice | solution.py:316
  17.6 3.3 %multiply_reduce_fusion.1 = f32[2048]{0:T(1024)S(1)} fusion(bf16[2048,1024]{1,0:T(8,128)(2,1)} %param.5), kind=kLoop, calls=%fused_computation.1 | loop fusion | flops 6289408 | bytes 4202496 | tf_op jit(solution)/shard_map/reduce_sum | solution.py:292
  20.9 0.3 multiply_reduce_fusion.2
  21.2 2.6 %add_reduce_fusion.1 = f32[512]{0:T(512)S(1)} fusion(bf16[2048,1024]{1,0:T(8,128)(2,1)S(1)} %copy-done, bf16[512,1024]{1,0:T(8,128)(2,1)S(1)} %copy-done.1, f32[2048]{0:T(1024)S(1)} %multiply_reduce_fusion.1, f32[512]{0:T(512)S(1)} %multiply_reduce_fusion.2), kind=kOutput, calls=%fused_computation.4 | convolution fusion | flops 2151677440 | bytes 5255168 | tf_op jit(solution)/shard_map/dot_general | solution.py:290
  23.8 0.0 collective-permute-done
  23.8 3.1 %multiply_reduce_fusion = f32[2048]{0:T(1024)S(1)} fusion(bf16[2048,1024]{1,0:T(8,128)(2,1)} %collective-permute-done), kind=kLoop, calls=%fused_computation | loop fusion | flops 6289408 | bytes 4202496 | tf_op jit(solution)/shard_map/reduce_sum | solution.py:292
  26.9 4.8 %add_reduce_fusion = f32[512]{0:T(512)S(1)} fusion(f32[2048]{0:T(1024)S(1)} %multiply_reduce_fusion, f32[512]{0:T(512)S(1)} %multiply_reduce_fusion.2, bf16[2048,1024]{1,0:T(8,128)(2,1)} %collective-permute-done, bf16[512,1024]{1,0:T(8,128)(2,1)S(1)} %copy-done.1), kind=kOutput, calls=%fused_computation.3 | convolution fusion | flops 2151677440 | bytes 5255168 | tf_op jit(solution)/shard_map/dot_general | solution.py:290
  31.7 0.6 minimum_multiply_fusion
  32.3 5.3 %all-to-all-done.recv_ref = bf16[16,272,128]{2,1,0:T(8,128)(2,1)S(1)} async-done(((bf16[16,272,128]{2,1,0:T(8,128)(2,1)}), bf16[16,272,128]{2,1,0:T(8,128)(2,1)S(1)}, u32[]{:S(2)}, u32[]{:S(2)}) %all-to-all-start) | async-done | bytes 1114144 | tf_op jit(solution)/shard_map/all_to_all | solution.py:309
  37.6 3.0 %sums_first.1 = (f32[272,512]{1,0:T(8,128)S(1)}, f32[8,128]{1,0:T(8,128)S(1)}) custom-call(s32[10]{0:T(128)S(1)} %stack.43.where_ref, bf16[16,272,128]{2,1,0:T(8,128)(2,1)S(1)} %all-to-all-done.recv_ref), custom_call_target="tpu_custom_call" | custom-call | flops 2281701376 | bytes 1114112 | tf_op jit(solution)/shard_map/sums_first/pallas_call | solution.py:164
  40.7 4.2 %sums_last.1 = (s16[512,256]{1,0:T(8,128)(2,1)S(1)}, f32[1]{0:T(128)}) custom-call(s32[10]{0:T(128)S(1)} %stack.43.where_ref, f32[1]{0:T(128)} %bitcast.2.least_ref, bf16[16,272,128]{2,1,0:T(8,128)(2,1)S(1)} %collective-permute-done.1.recv_ref, f32[272,512]{1,0:T(8,128)S(1)} %get-tuple-element.18.given_ref, f32[8,128]{1,0:T(8,128)S(1)} %get-tuple-element.19.given_peak_ref, ...), custom_call_target="tpu_custom_call" | custom-call | flops 2281701376 | bytes 1114112 | tf_op jit(solution)/shard_map/sums_last/pallas_call | solution.py:180
  44.9 2.1 %collective-permute-start.4 = (s16[512,256]{1,0:T(8,128)(2,1)S(1)}, s16[512,256]{1,0:T(8,128)(2,1)S(1)}, u32[]{:S(2)}, u32[]{:S(2)}) collective-permute-start(s16[512,256]{1,0:T(8,128)(2,1)S(1)} %get-tuple-element.22.refs_0_), channel_id=1, source_target_pairs={{0,4},{4,0},{1,5},{5,1},{2,6},{6,2},{3,7},{7,3},{8,12},{12,8},{9,1... | collective-permute-start | bytes 786440 | tf_op jit(solution)/shard_map/ppermute | solution.py:269
  47.0 2.8 %collective-permute-start.12 = (s16[512,256]{1,0:T(8,128)(2,1)S(1)}, s16[512,256]{1,0:T(8,128)(2,1)S(1)}, u32[]{:S(2)}, u32[]{:S(2)}) collective-permute-start(s16[512,256]{1,0:T(8,128)(2,1)S(1)} %get-tuple-element.22.refs_0_), channel_id=1, source_target_pairs={{0,8},{8,16},{16,24},{24,0},{1,9},{9,17},{17,25},{25,1},{2,10},{10... | collective-permute-start | bytes 786440 | tf_op jit(solution)/shard_map/ppermute | solution.py:269
  49.8 1.1 %collective-permute-start.7 = (s16[512,256]{1,0:T(8,128)(2,1)S(1)}, s16[512,256]{1,0:T(8,128)(2,1)S(1)}, u32[]{:S(2)}, u32[]{:S(2)}) collective-permute-start(s16[512,256]{1,0:T(8,128)(2,1)S(1)} %get-tuple-element.22.refs_0_), channel_id=1, source_target_pairs={{0,24},{8,0},{16,8},{24,16},{1,25},{9,1},{17,9},{25,17},{2,26},{10... | collective-permute-start | bytes 786440 | tf_op jit(solution)/shard_map/ppermute | solution.py:269
  51.0 0.8 collective-permute-start.17
  51.7 0.5 collective-permute-start.2
  52.2 1.8 %collective-permute-done.4.refs_2_ = s16[512,256]{1,0:T(8,128)(2,1)S(1)} collective-permute-done((s16[512,256]{1,0:T(8,128)(2,1)S(1)}, s16[512,256]{1,0:T(8,128)(2,1)S(1)}, u32[]{:S(2)}, u32[]{:S(2)}) %collective-permute-start.4) | collective-permute-done | bytes 262176 | tf_op jit(solution)/shard_map/ppermute | solution.py:269
  54.0 0.9 collective-permute-start.5
  54.9 3.3 %collective-permute-done.12.refs_0_ = s16[512,256]{1,0:T(8,128)(2,1)S(1)} collective-permute-done((s16[512,256]{1,0:T(8,128)(2,1)S(1)}, s16[512,256]{1,0:T(8,128)(2,1)S(1)}, u32[]{:S(2)}, u32[]{:S(2)}) %collective-permute-start.12) | collective-permute-done | bytes 262176 | tf_op jit(solution)/shard_map/ppermute | solution.py:269
  58.2 0.8 collective-permute-start.14
  58.9 4.4 %collective-permute-done.7.refs_2_ = s16[512,256]{1,0:T(8,128)(2,1)S(1)} collective-permute-done((s16[512,256]{1,0:T(8,128)(2,1)S(1)}, s16[512,256]{1,0:T(8,128)(2,1)S(1)}, u32[]{:S(2)}, u32[]{:S(2)}) %collective-permute-start.7) | collective-permute-done | bytes 262176 | tf_op jit(solution)/shard_map/ppermute | solution.py:269
  63.3 0.7 collective-permute-start.10
  64.0 0.0 collective-permute-done.17.refs_1_
  64.0 0.3 collective-permute-start.8
  64.3 10.2 %collective-permute-done.2.refs_2_ = s16[512,256]{1,0:T(8,128)(2,1)S(1)} collective-permute-done((s16[512,256]{1,0:T(8,128)(2,1)S(1)}, s16[512,256]{1,0:T(8,128)(2,1)S(1)}, u32[]{:S(2)}, u32[]{:S(2)}) %collective-permute-start.2) | collective-permute-done | bytes 262176 | tf_op jit(solution)/shard_map/ppermute | solution.py:269
  74.5 0.3 collective-permute-start.13
  74.9 0.7 collective-permute-start.16
  75.5 0.0 collective-permute-done.14.refs_1_
  75.6 1.7 %collective-permute-start.15 = (s16[512,256]{1,0:T(8,128)(2,1)S(1)}, s16[512,256]{1,0:T(8,128)(2,1)S(1)}, u32[]{:S(2)}, u32[]{:S(2)}) collective-permute-start(s16[512,256]{1,0:T(8,128)(2,1)S(1)} %collective-permute-done.14.refs_1_), channel_id=1, source_target_pairs={{0,4},{4,0},{1,5},{5,1},{2,6},{6,2},{3,7},{7,3},{8,12},{12,8},{9,1... | collective-permute-start | bytes 786440 | tf_op jit(solution)/shard_map/ppermute | solution.py:269
  77.2 0.3 collective-permute-start.3
  77.6 4.0 %collective-permute-start.6 = (s16[512,256]{1,0:T(8,128)(2,1)S(1)}, s16[512,256]{1,0:T(8,128)(2,1)S(1)}, u32[]{:S(2)}, u32[]{:S(2)}) collective-permute-start(s16[512,256]{1,0:T(8,128)(2,1)S(1)} %collective-permute-done.5.refs_3_), channel_id=1, source_target_pairs={{0,16},{8,24},{16,0},{24,8},{1,17},{9,25},{17,1},{25,9},{2,18},{10... | collective-permute-start | bytes 786440 | tf_op jit(solution)/shard_map/ppermute | solution.py:269
  81.6 2.1 %collective-permute-done.13.refs_0_ = s16[512,256]{1,0:T(8,128)(2,1)S(1)} collective-permute-done((s16[512,256]{1,0:T(8,128)(2,1)S(1)}, s16[512,256]{1,0:T(8,128)(2,1)S(1)}, u32[]{:S(2)}, u32[]{:S(2)}) %collective-permute-start.13) | collective-permute-done | bytes 262176 | tf_op jit(solution)/shard_map/ppermute | solution.py:269
  83.7 0.3 collective-permute-start.11
  84.1 0.0 collective-permute-done.16.refs_3_
  84.1 0.7 collective-permute-start.9
  84.7 3.0 %spread.4.refs_4_ = f32[2048,1024]{1,0:T(8,128)} custom-call(s32[10]{0:T(128)S(1)} %stack.43.where_ref, f32[1]{0:T(128)} %get-tuple-element.21.peak_ref, s16[512,256]{1,0:T(8,128)(2,1)S(1)} %get-tuple-element.22.refs_0_, s16[512,256]{1,0:T(8,128)(2,1)S(1)} %collective-permute-done.17.refs_1_, s16[512,256]{1,0:T(8,128)(2,1)S(1)} %collective-permute-done.4.refs_2_, ...), custom_call_target="tpu_custom_call" | custom-call | flops 4194304 | bytes 3145728 | tf_op jit(solution)/shard_map/spread/pallas_call | solution.py:238
  87.7 3.0 %spread.5.refs_4_ = f32[2048,1024]{1,0:T(8,128)} custom-call(s32[10]{0:T(128)S(1)} %stack.43.where_ref, f32[1]{0:T(128)} %get-tuple-element.21.peak_ref, s16[512,256]{1,0:T(8,128)(2,1)S(1)} %collective-permute-done.12.refs_0_, s16[512,256]{1,0:T(8,128)(2,1)S(1)} %collective-permute-done.14.refs_1_, ...), custom_call_target="tpu_custom_call", output_to_operand_aliasing={{}: (6, {})} | custom-call | flops 4194304 | bytes 3145728 | tf_op jit(solution)/shard_map/spread/pallas_call | solution.py:238
  90.7 0.0 collective-permute-done.15.refs_1_
  90.8 3.0 %spread.6.refs_5_ = f32[2048,1024]{1,0:T(8,128)} custom-call(s32[10]{0:T(128)S(1)} %stack.43.where_ref, f32[1]{0:T(128)} %get-tuple-element.21.peak_ref, s16[512,256]{1,0:T(8,128)(2,1)S(1)} %collective-permute-done.13.refs_0_, s16[512,256]{1,0:T(8,128)(2,1)S(1)} %collective-permute-done.15.refs_1_, ...), custom_call_target="tpu_custom_call", output_to_operand_aliasing={{}: (6, {})} | custom-call | flops 4194304 | bytes 3145728 | tf_op jit(solution)/shard_map/spread/pallas_call | solution.py:238
  93.8 1.2 %collective-permute-done.3.refs_0_ = s16[512,256]{1,0:T(8,128)(2,1)S(1)} collective-permute-done((s16[512,256]{1,0:T(8,128)(2,1)S(1)}, s16[512,256]{1,0:T(8,128)(2,1)S(1)}, u32[]{:S(2)}, u32[]{:S(2)}) %collective-permute-start.3) | collective-permute-done | bytes 262176 | tf_op jit(solution)/shard_map/ppermute | solution.py:269
  95.0 1.9 %collective-permute-done.11.refs_4_ = s16[256,256]{1,0:T(8,128)(2,1)S(1)} collective-permute-done((s16[256,256]{1,0:T(8,128)(2,1)S(1)}, s16[256,256]{1,0:T(8,128)(2,1)S(1)}, u32[]{:S(2)}, u32[]{:S(2)}) %collective-permute-start.11) | collective-permute-done | bytes 131104 | tf_op jit(solution)/shard_map/ppermute | solution.py:269
  96.9 3.0 %spread.7 = f32[2048,1024]{1,0:T(8,128)} custom-call(s32[10]{0:T(128)S(1)} %stack.43.where_ref, f32[1]{0:T(128)} %get-tuple-element.21.peak_ref, s16[512,256]{1,0:T(8,128)(2,1)S(1)} %collective-permute-done.3.refs_0_, s16[512,256]{1,0:T(8,128)(2,1)S(1)} %collective-permute-done.6.refs_1_, ...), custom_call_target="tpu_custom_call", output_to_operand_aliasing={{}: (7, {})} | custom-call | flops 4194304 | bytes 3145728 | tf_op jit(solution)/shard_map/spread/pallas_call | solution.py:238
  (12 shorter events, 0.0 us)
Async XLA Ops:
  3.2 20.6 %collective-permute-start = (bf16[2048,1024]{1,0:T(8,128)(2,1)}, bf16[2048,1024]{1,0:T(8,128)(2,1)}, u32[]{:S(2)}, u32[]{:S(2)}) collective-permute-start(bf16[2048,1024]{1,0:T(8,128)(2,1)} %param.5), channel_id=1, source_target_pairs={{0,1},{1,0},{2,3},{3,2},{4,5},{5,4},{6,7},{7,6},{8,9},{9,8},{10,11... | collective-permute-start | bytes 12582920 | tf_op jit(solution)/shard_map/ppermute | solution.py:310
  3.7 33.9 %all-to-all-start = ((bf16[16,272,128]{2,1,0:T(8,128)(2,1)}), bf16[16,272,128]{2,1,0:T(8,128)(2,1)S(1)}, u32[]{:S(2)}, u32[]{:S(2)}) async-start(bf16[16,272,128]{2,1,0:T(8,128)(2,1)} %pack.1), calls=%async_computation | async-start | bytes 2228224 | tf_op jit(solution)/shard_map/all_to_all | solution.py:309
  11.6 9.2 %copy-start.1 = (bf16[512,1024]{1,0:T(8,128)(2,1)S(1)}, bf16[512,1024]{1,0:T(8,128)(2,1)}, u32[]{:S(2)}) copy-start(bf16[512,1024]{1,0:T(8,128)(2,1)} %points_ref.1) | copy-start | bytes 3145732
  16.4 4.8 %copy-start = (bf16[2048,1024]{1,0:T(8,128)(2,1)S(1)}, bf16[2048,1024]{1,0:T(8,128)(2,1)}, u32[]{:S(2)}) copy-start(bf16[2048,1024]{1,0:T(8,128)(2,1)} %param.5) | copy-start | bytes 12582916
  37.6 3.1 %collective-permute-start.1 = (bf16[16,272,128]{2,1,0:T(8,128)(2,1)S(1)}, bf16[16,272,128]{2,1,0:T(8,128)(2,1)S(1)}, u32[]{:S(2)}, u32[]{:S(2)}) collective-permute-start(bf16[16,272,128]{2,1,0:T(8,128)(2,1)S(1)} %all-to-all-done.recv_ref), channel_id=1, source_target_pairs={{0,1},{1,0},{2,3},{3,2},{4,5},{5,4},{6,7},{7,6},{8,9},{9,8},{10,11... | collective-permute-start | bytes 3342344 | tf_op jit(solution)/shard_map/ppermute | solution.py:319
  44.9 9.1 %collective-permute-start.4 = (s16[512,256]{1,0:T(8,128)(2,1)S(1)}, s16[512,256]{1,0:T(8,128)(2,1)S(1)}, u32[]{:S(2)}, u32[]{:S(2)}) collective-permute-start(s16[512,256]{1,0:T(8,128)(2,1)S(1)} %get-tuple-element.22.refs_0_), channel_id=1, source_target_pairs={{0,4},{4,0},{1,5},{5,1},{2,6},{6,2},{3,7},{7,3},{8,12},{12,8},{9,1... | collective-permute-start | bytes 786440 | tf_op jit(solution)/shard_map/ppermute | solution.py:269
  47.0 11.2 %collective-permute-start.12 = (s16[512,256]{1,0:T(8,128)(2,1)S(1)}, s16[512,256]{1,0:T(8,128)(2,1)S(1)}, u32[]{:S(2)}, u32[]{:S(2)}) collective-permute-start(s16[512,256]{1,0:T(8,128)(2,1)S(1)} %get-tuple-element.22.refs_0_), channel_id=1, source_target_pairs={{0,8},{8,16},{16,24},{24,0},{1,9},{9,17},{17,25},{25,1},{2,10},{10... | collective-permute-start | bytes 786440 | tf_op jit(solution)/shard_map/ppermute | solution.py:269
  49.8 13.5 %collective-permute-start.7 = (s16[512,256]{1,0:T(8,128)(2,1)S(1)}, s16[512,256]{1,0:T(8,128)(2,1)S(1)}, u32[]{:S(2)}, u32[]{:S(2)}) collective-permute-start(s16[512,256]{1,0:T(8,128)(2,1)S(1)} %get-tuple-element.22.refs_0_), channel_id=1, source_target_pairs={{0,24},{8,0},{16,8},{24,16},{1,25},{9,1},{17,9},{25,17},{2,26},{10... | collective-permute-start | bytes 786440 | tf_op jit(solution)/shard_map/ppermute | solution.py:269
  51.0 13.0 %collective-permute-start.17 = (s16[512,256]{1,0:T(8,128)(2,1)S(1)}, s16[512,256]{1,0:T(8,128)(2,1)S(1)}, u32[]{:S(2)}, u32[]{:S(2)}) collective-permute-start(s16[512,256]{1,0:T(8,128)(2,1)S(1)} %get-tuple-element.22.refs_0_), channel_id=1, source_target_pairs={{0,2},{2,0},{1,3},{3,1},{4,6},{6,4},{5,7},{7,5},{8,10},{10,8},{9,1... | collective-permute-start | bytes 786440 | tf_op jit(solution)/shard_map/ppermute | solution.py:269
  51.7 22.8 %collective-permute-start.2 = (s16[512,256]{1,0:T(8,128)(2,1)S(1)}, s16[512,256]{1,0:T(8,128)(2,1)S(1)}, u32[]{:S(2)}, u32[]{:S(2)}) collective-permute-start(s16[512,256]{1,0:T(8,128)(2,1)S(1)} %get-tuple-element.22.refs_0_), channel_id=1, source_target_pairs={{0,16},{8,24},{16,0},{24,8},{1,17},{9,25},{17,1},{25,9},{2,18},{10... | collective-permute-start | bytes 786440 | tf_op jit(solution)/shard_map/ppermute | solution.py:269
  54.0 20.9 %collective-permute-start.5 = (s16[512,256]{1,0:T(8,128)(2,1)S(1)}, s16[512,256]{1,0:T(8,128)(2,1)S(1)}, u32[]{:S(2)}, u32[]{:S(2)}) collective-permute-start(s16[512,256]{1,0:T(8,128)(2,1)S(1)} %collective-permute-done.4.refs_2_), channel_id=1, source_target_pairs={{0,2},{2,0},{1,3},{3,1},{4,6},{6,4},{5,7},{7,5},{8,10},{10,8},{9,1... | collective-permute-start | bytes 786440 | tf_op jit(solution)/shard_map/ppermute | solution.py:269
  58.2 17.4 %collective-permute-start.14 = (s16[512,256]{1,0:T(8,128)(2,1)S(1)}, s16[512,256]{1,0:T(8,128)(2,1)S(1)}, u32[]{:S(2)}, u32[]{:S(2)}) collective-permute-start(s16[512,256]{1,0:T(8,128)(2,1)S(1)} %collective-permute-done.12.refs_0_), channel_id=1, source_target_pairs={{0,2},{2,0},{1,3},{3,1},{4,6},{6,4},{5,7},{7,5},{8,10},{10,8},{9,1... | collective-permute-start | bytes 786440 | tf_op jit(solution)/shard_map/ppermute | solution.py:269
  63.3 13.9 %collective-permute-start.10 = (s16[512,256]{1,0:T(8,128)(2,1)S(1)}, s16[512,256]{1,0:T(8,128)(2,1)S(1)}, u32[]{:S(2)}, u32[]{:S(2)}) collective-permute-start(s16[512,256]{1,0:T(8,128)(2,1)S(1)} %collective-permute-done.7.refs_2_), channel_id=1, source_target_pairs={{0,2},{2,0},{1,3},{3,1},{4,6},{6,4},{5,7},{7,5},{8,10},{10,8},{9,1... | collective-permute-start | bytes 786440 | tf_op jit(solution)/shard_map/ppermute | solution.py:269
  64.0 13.6 %collective-permute-start.8 = (s16[512,256]{1,0:T(8,128)(2,1)S(1)}, s16[512,256]{1,0:T(8,128)(2,1)S(1)}, u32[]{:S(2)}, u32[]{:S(2)}) collective-permute-start(s16[512,256]{1,0:T(8,128)(2,1)S(1)} %collective-permute-done.7.refs_2_), channel_id=1, source_target_pairs={{0,4},{4,0},{1,5},{5,1},{2,6},{6,2},{3,7},{7,3},{8,12},{12,8},{9,1... | collective-permute-start | bytes 786440 | tf_op jit(solution)/shard_map/ppermute | solution.py:269
  74.5 9.2 %collective-permute-start.13 = (s16[512,256]{1,0:T(8,128)(2,1)S(1)}, s16[512,256]{1,0:T(8,128)(2,1)S(1)}, u32[]{:S(2)}, u32[]{:S(2)}) collective-permute-start(s16[512,256]{1,0:T(8,128)(2,1)S(1)} %collective-permute-done.12.refs_0_), channel_id=1, source_target_pairs={{0,4},{4,0},{1,5},{5,1},{2,6},{6,2},{3,7},{7,3},{8,12},{12,8},{9,1... | collective-permute-start | bytes 786440 | tf_op jit(solution)/shard_map/ppermute | solution.py:269
  74.9 9.2 %collective-permute-start.16 = (s16[512,256]{1,0:T(8,128)(2,1)S(1)}, s16[512,256]{1,0:T(8,128)(2,1)S(1)}, u32[]{:S(2)}, u32[]{:S(2)}) collective-permute-start(s16[512,256]{1,0:T(8,128)(2,1)S(1)} %collective-permute-done.2.refs_2_), channel_id=1, source_target_pairs={{0,2},{2,0},{1,3},{3,1},{4,6},{6,4},{5,7},{7,5},{8,10},{10,8},{9,1... | collective-permute-start | bytes 786440 | tf_op jit(solution)/shard_map/ppermute | solution.py:269
  75.6 15.2 %collective-permute-start.15 = (s16[512,256]{1,0:T(8,128)(2,1)S(1)}, s16[512,256]{1,0:T(8,128)(2,1)S(1)}, u32[]{:S(2)}, u32[]{:S(2)}) collective-permute-start(s16[512,256]{1,0:T(8,128)(2,1)S(1)} %collective-permute-done.14.refs_1_), channel_id=1, source_target_pairs={{0,4},{4,0},{1,5},{5,1},{2,6},{6,2},{3,7},{7,3},{8,12},{12,8},{9,1... | collective-permute-start | bytes 786440 | tf_op jit(solution)/shard_map/ppermute | solution.py:269
  77.2 17.7 %collective-permute-start.3 = (s16[512,256]{1,0:T(8,128)(2,1)S(1)}, s16[512,256]{1,0:T(8,128)(2,1)S(1)}, u32[]{:S(2)}, u32[]{:S(2)}) collective-permute-start(s16[512,256]{1,0:T(8,128)(2,1)S(1)} %collective-permute-done.2.refs_2_), channel_id=1, source_target_pairs={{0,4},{4,0},{1,5},{5,1},{2,6},{6,2},{3,7},{7,3},{8,12},{12,8},{9,1... | collective-permute-start | bytes 786440 | tf_op jit(solution)/shard_map/ppermute | solution.py:269
  77.6 19.3 %collective-permute-start.6 = (s16[512,256]{1,0:T(8,128)(2,1)S(1)}, s16[512,256]{1,0:T(8,128)(2,1)S(1)}, u32[]{:S(2)}, u32[]{:S(2)}) collective-permute-start(s16[512,256]{1,0:T(8,128)(2,1)S(1)} %collective-permute-done.5.refs_3_), channel_id=1, source_target_pairs={{0,16},{8,24},{16,0},{24,8},{1,17},{9,25},{17,1},{25,9},{2,18},{10... | collective-permute-start | bytes 786440 | tf_op jit(solution)/shard_map/ppermute | solution.py:269
  83.7 13.1 %collective-permute-start.11 = (s16[256,256]{1,0:T(8,128)(2,1)S(1)}, s16[256,256]{1,0:T(8,128)(2,1)S(1)}, u32[]{:S(2)}, u32[]{:S(2)}) collective-permute-start(s16[256,256]{1,0:T(8,128)(2,1)S(1)} %slice.9), channel_id=1, source_target_pairs={{0,4},{4,0},{1,5},{5,1},{2,6},{6,2},{3,7},{7,3},{8,12},{12,8},{9,1... | collective-permute-start | bytes 393224 | tf_op jit(solution)/shard_map/ppermute | solution.py:269
  84.1 12.8 %collective-permute-start.9 = (s16[256,256]{1,0:T(8,128)(2,1)S(1)}, s16[256,256]{1,0:T(8,128)(2,1)S(1)}, u32[]{:S(2)}, u32[]{:S(2)}) collective-permute-start(s16[256,256]{1,0:T(8,128)(2,1)S(1)} %slice.8), channel_id=1, source_target_pairs={{0,2},{2,0},{1,3},{3,1},{4,6},{6,4},{5,7},{7,5},{8,10},{10,8},{9,1... | collective-permute-start | bytes 393224 | tf_op jit(solution)/shard_map/ppermute | solution.py:269
